TPU v7x, 256 devices: a whole 4x4x8 slice. The times are simulated.
256 devices in a mesh: dp: 64 (over y, x_hi, z), mp: 4 (over x_lo, core).
Axes of the slice: x: 4 (x_hi: 2, x_lo: 2; x = x_hi * 2 + x_lo), y: 4, z: 8, core: 2. Of those that a mesh axis runs over, the one named last changes fastest.
Arguments:
- picture_skip_activations: bfloat16 [131072, 1152], P('dp'), as said below
- caption_closing_activations: bfloat16 [512, 1152], P('dp'), as said below
- normaliser_multipliers: float32 [3, 1152], replicated, may hold values from 0.1 to 1.9
- widening_matrix: bfloat16 [1152, 4304], P('dp', 'mp'), may hold values from -0.1875 to 0.1875
- contracting_matrix: bfloat16 [4304, 1152], P('mp', 'dp'), as said below
- caption_mapping_matrix: bfloat16 [1152, 1152], replicated, as said below
- sharpness_factor: float32 [1], replicated, may hold values from 8 to 32
- score_offset_term: float32 [1], replicated, may hold values from -8 to -3
Outputs:
- row_loss: float32 [512], P('dp')
- col_loss: float32 [512], P('dp')
Inputs may be any that keep to these rules, and one draw needn't show every extreme that they name: `picture_skip_activations`: entries lie within -8 and 8. `caption_closing_activations`: entries lie within -8 and 8. `contracting_matrix`: entries are at most 4.4 / sqrt(4304) in magnitude. `caption_mapping_matrix`: diagonal entries lie within 1 - 2.1 / sqrt(1152) and 1 + 2.1 / sqrt(1152), the others within -2.1 / sqrt(1152) and 2.1 / sqrt(1152).
All inputs are finite; a program needn't handle non-finite values.
Results may differ from a plain program's by a relative error of at most 0.01.
Values may be sent and summed in bfloat16 or wider, within the bound.
No kernel may reach another device: no remote copies, remote signals or barrier semaphores. Data moves between devices by JAX's collectives and lax.ppermute only.
A program may use at most 128 MiB of HBM per device.

v0:
```python
import jax
import jax.numpy as jnp
from jax import lax
from jax.experimental import pallas as pl
from jax.experimental.pallas import tpu as pltpu
from jax.sharding import Mesh
from jax.sharding import PartitionSpec as P


D = 1152
HID = 1152
PATCHES = 256
PAIRS = 512
DP = ("y", "xh", "z")
XS = ("xh", "xl")
ALL = ("y", "xh", "z", "xl", "c")
W1A, W1B, W2A, W2B, TX = 80, 64, 64, 80, 16
BF = jnp.bfloat16
F32 = jnp.float32


def shifted(array, axes, by, size=4):
    return lax.ppermute(array, axes, [(i, (i + by) % size) for i in range(size)])


def small_ring(block, cut, axes):
    right, left = shifted(block, axes, 1), shifted(block, axes, -1)
    far1, far2 = shifted(right[:cut], axes, 1), shifted(left[cut:], axes, -1)
    first = jnp.stack([block[:cut], right[:cut], far1, left[:cut]])
    return first, jnp.stack([block[cut:], right[cut:], far2, left[cut:]])


def large_ring(block, axes):
    right = shifted(block, axes, 1)
    left = shifted(block, axes, -1)
    far_r = shifted(right[:2], axes, 1)
    far_l = shifted(left[2:], axes, -1)
    return block, right, left, far_r, far_l


def gathered_along_z(block):
    one_r, one_l = shifted(block, "z", 1, 8), shifted(block, "z", -1, 8)
    two_r, two_l = shifted(block, "z", 2, 8), shifted(block, "z", -2, 8)
    three_r, three_l = shifted(two_r, "z", 1, 8), shifted(two_l, "z", -1, 8)
    four = shifted(two_r, "z", 2, 8)
    z = lax.axis_index("z")
    out = jnp.zeros((8, *block.shape), block.dtype)
    pieces = ((0, block), (-1, one_r), (1, one_l), (-2, two_r), (2, two_l), (-3, three_r), (3, three_l), (4, four))
    for by, piece in pieces:
        out = lax.dynamic_update_slice(out, piece[None], (lax.rem(z + by + 8, 8), 0, 0))
    return out


def layer_norm(values, norm_gain):
    average = jnp.mean(values, axis=-1, keepdims=True)
    centred = values - average
    spread = jnp.mean(centred * centred, axis=-1, keepdims=True)
    return centred * lax.rsqrt(spread + 1e-06) * norm_gain


def place():
    x = lax.axis_index("xh") * 2 + lax.axis_index("xl")
    return x, lax.axis_index("y")


def each_piece(a_refs, b_refs, write):
    x, y = place()

    def visit(ref, n, i, j, half):
        xk, yk = (i, j) if half == 0 else (j, i)
        write(half, ref, n, lax.rem(x - xk + 4, 4), lax.rem(y - yk + 4, 4))

    def whole(i, _):
        for half, refs in enumerate((a_refs, b_refs)):
            for ref, j in ((refs[0], 0), (refs[1], 1), (refs[2], 3)):
                visit(ref, i, i, j, half)
        return 0

    def halves(u, _):
        for half, refs in enumerate((a_refs, b_refs)):
            visit(refs[3], u, u, 2, half)
            visit(refs[4], u, u + 2, 2, half)
        return 0

    lax.fori_loop(0, 4, whole, 0)
    lax.fori_loop(0, 2, halves, 0)


def put_in_order(rows, dst, ref, half, n, xx, yy):
    at = pl.multiple_of((yy * 2 + xx // 2) * 144 + half * rows[0], 16)
    dst[lax.rem(xx, 2), pl.ds(at, rows[half]), :] = ref[n, 0 : rows[half], :]


ROWS = 512


def gelu(v):
    inner = 0.7978845608028654 * (v + 0.044715 * (v * v * v))
    return (0.5 * v * (1.0 + jnp.tanh(inner))).astype(BF)


def norm_kernel(x_ref, gain_ref, normed_ref, own_ref, sem):
    first = pl.multiple_of(lax.axis_index("xl") * 1024, 1024)
    copy = pltpu.make_async_copy(x_ref.at[pl.ds(first, 1024), :], normed_ref, sem)
    copy.start()
    copy.wait()
    half = pl.multiple_of(lax.axis_index("c") * 512, 512)
    gain = gain_ref[...]

    def keep(r, _):
        rows = pl.multiple_of(r * 64, 64)
        own_ref[pl.ds(rows, 64), :] = normed_ref[pl.ds(half + rows, 64), :]
        return 0

    def norm(r, _):
        rows = pl.ds(pl.multiple_of(r * 32, 32), 32)
        normed_ref[rows, :] = layer_norm(normed_ref[rows, :].astype(F32), gain).astype(BF)
        return 0

    lax.fori_loop(0, 8, keep, 0)
    lax.fori_loop(0, 32, norm, 0)


def widen_kernel(normed_ref, *refs):
    a_refs, b_refs, (h, texts, w1) = refs[:5], refs[5:10], refs[10:]
    rows = (W1A, W1B)

    def write(half, ref, n, xx, yy):
        put_in_order(rows, w1, ref, half, n, xx, yy)
        at = pl.multiple_of((yy * 4 + xx) * 32 + half * TX, 16)
        texts[pl.ds(at, TX), :] = ref[n, rows[half] : rows[half] + TX, :]

    each_piece(a_refs, b_refs, write)

    def widen(t, _):
        k = t // 2
        rows = pl.ds(pl.multiple_of(lax.rem(t, 2) * ROWS, ROWS), ROWS)
        h[k, rows, :] = gelu(jnp.dot(normed_ref[rows, :], w1[k], preferred_element_type=F32))
        return 0

    lax.fori_loop(0, 4, widen, 0)


def contracted(h, w2, half, out_ref):
    def step(r, _):
        rows = pl.ds(pl.multiple_of(half * 512 + r * 256, 256), 256)
        total = None
        for k in range(2):
            part = lax.dot_general(
                h[k, rows, :], w2[k], (((1,), (1,)), ((), ())), preferred_element_type=F32
            )
            total = part if total is None else total + part
        out_ref[pl.ds(pl.multiple_of(r * 256, 256), 256), :] = total.astype(out_ref.dtype)
        return 0

    lax.fori_loop(0, 2, step, 0)


def contract_sent_kernel(h, *refs):
    a_refs, b_refs, (sent_ref, w2) = refs[:5], refs[5:10], refs[10:]

    def write(half, ref, n, xx, yy):
        put_in_order((W2A, W2B), w2, ref, half, n, xx, yy)

    each_piece(a_refs, b_refs, write)
    contracted(h, w2, 1 - lax.axis_index("c"), sent_ref)


def contract_own_kernel(h, w2, own_ref):
    contracted(h, w2, lax.axis_index("c"), own_ref)


def text_kernel(gain_ref, map_ref, rows_ref, out_ref):
    gain = gain_ref[...]

    def embed(r, _):
        rows = pl.ds(pl.multiple_of(r * 128, 128), 128)
        normed = layer_norm(rows_ref[rows, :].astype(F32), gain).astype(BF)
        vector = jnp.dot(normed, map_ref[...], preferred_element_type=F32)
        length = jnp.sqrt(jnp.sum(vector * vector, axis=-1, keepdims=True))
        out_ref[rows, :] = (vector / jnp.maximum(length, 1.0)).astype(BF)
        return 0

    lax.fori_loop(0, PAIRS // 128, embed, 0)


def last_kernel(scale_ref, shift_ref, x_ref, own_ref, recv_ref, gain_ref, text_ref, out_ref):
    gain = gain_ref[...]
    pooled = []
    for k in range(2):

        def pool(r, total, k=k):
            rows = pl.ds(pl.multiple_of(k * PATCHES + r * 64, 64), 64)
            v = x_ref[rows, :].astype(F32) + (own_ref[rows, :] + recv_ref[rows, :].astype(F32))
            final = layer_norm(v, gain)
            return total + jnp.sum(final.reshape(8, 8, D), axis=0)

        total = lax.fori_loop(0, PATCHES // 64, pool, jnp.zeros((8, D), F32))
        pooled.append(jnp.sum(total, axis=0, keepdims=True) * (1.0 / PATCHES))
    vector = jnp.concatenate(pooled + [jnp.zeros((6, D), F32)], axis=0)
    length = jnp.sqrt(jnp.sum(vector * vector, axis=-1, keepdims=True))
    emb = (vector / jnp.maximum(length, 1.0)).astype(BF)
    scores = (
        lax.dot_general(text_ref[...], emb, (((1,), (1,)), ((), ())), preferred_element_type=F32)
        * scale_ref[0]
        + shift_ref[0]
    )
    dp = lax.axis_index("y") * 16 + lax.axis_index("xh") * 8 + lax.axis_index("z")
    slot = lax.axis_index("xl") * 4 + lax.axis_index("c") * 2
    q = lax.broadcasted_iota(jnp.int32, (PAIRS, 8), 0)
    col = lax.broadcasted_iota(jnp.int32, (PAIRS, 8), 1)
    q_dp, q_slot = (q // 64) * 8 + (q // 4) % 8, ((q // 32) % 2) * 4 + q % 4
    own_pair = (q_dp == dp) & (q_slot == slot + col)
    value = jnp.where(own_pair, -scores, scores)
    terms = jnp.maximum(value, 0.0) + jnp.log1p(jnp.exp(-jnp.abs(value)))
    terms = jnp.where(col < 2, terms, 0.0)
    cols = jnp.sum(terms, axis=1, keepdims=True)
    rows = jnp.sum(terms, axis=0, keepdims=True)
    spread = jnp.where(q_slot == col, cols, 0.0)
    r = lax.broadcasted_iota(jnp.int32, (64, PAIRS), 0)
    c = lax.broadcasted_iota(jnp.int32, (64, PAIRS), 1)
    owner = jnp.where((c // 64) * 8 + (c // 4) % 8 == r, 1.0, 0.0)
    col_part = jnp.dot(owner, spread, precision=lax.Precision.HIGHEST, preferred_element_type=F32)
    mr = lax.broadcasted_iota(jnp.int32, (64, 8), 0)
    mc = lax.broadcasted_iota(jnp.int32, (64, 8), 1)
    row_part = jnp.where(mc == slot, rows[:, 0:1], jnp.where(mc == slot + 1, rows[:, 1:2], 0.0))
    row_part = jnp.where(mr == dp, row_part, 0.0)
    message = jnp.concatenate([col_part, row_part], axis=1)
    for m in range(4):
        out_ref[:, m, :] = message


ANY = pl.BlockSpec(memory_space=pl.ANY)
VM = pl.BlockSpec(memory_space=pltpu.VMEM)
SM = pl.BlockSpec(memory_space=pltpu.SMEM)


def on_device(
    picture_skip_activations,
    caption_closing_activations,
    normaliser_multipliers,
    widening_matrix,
    contracting_matrix,
    caption_mapping_matrix,
    sharpness_factor,
    score_offset_term,
):
    xl = lax.axis_index("xl")
    texts = lax.dynamic_slice_in_dim(caption_closing_activations, xl * 4, 4, 0)
    weights = jnp.concatenate([widening_matrix, contracting_matrix.T], axis=0)
    weights = jnp.pad(weights, ((0, 0), (0, HID - weights.shape[1])))
    shard = jnp.concatenate([weights, texts], axis=0)
    along_z = gathered_along_z(shard)
    w1 = along_z[:, :18].reshape(144, HID)
    w2 = along_z[:, 18:36].reshape(144, HID)
    tx = along_z[:, 36:].reshape(32, D)
    a = jnp.concatenate([w1[:W1A], tx[:TX], w2[:W2A]], axis=0)
    b = jnp.concatenate([w1[W1A:], tx[TX:], w2[W2A:]], axis=0)

    a1, a2 = small_ring(a, W1A + TX, XS)
    b1, b2 = small_ring(b, W1B + TX, "y")
    a1, b1 = large_ring(a1, "y"), large_ring(b1, XS)
    a2, b2 = large_ring(a2, "y"), large_ring(b2, XS)

    normed, own_rows = pl.pallas_call(
        norm_kernel,
        out_shape=(jax.ShapeDtypeStruct((1024, D), BF), jax.ShapeDtypeStruct((512, D), BF)),
        in_specs=[ANY, VM],
        out_specs=(VM, VM),
        scratch_shapes=[pltpu.SemaphoreType.DMA],
        name="norm",
        cost_estimate=pl.CostEstimate(flops=20 * 1024 * D, transcendentals=0, bytes_accessed=6 << 20),
        compiler_params=pltpu.CompilerParams(vmem_limit_bytes=8 << 20),
    )(picture_skip_activations, normaliser_multipliers[0:1])

    cost = pl.CostEstimate(flops=4 * 1024 * D * HID, transcendentals=0, bytes_accessed=12 << 20)
    units, texts = pl.pallas_call(
        widen_kernel,
        out_shape=(jax.ShapeDtypeStruct((2, 1024, HID), BF), jax.ShapeDtypeStruct((PAIRS, D), BF)),
        in_specs=[VM] * 11,
        out_specs=(VM, VM),
        scratch_shapes=[pltpu.VMEM((2, D, HID), BF)],
        name="widen",
        cost_estimate=cost,
        compiler_params=pltpu.CompilerParams(vmem_limit_bytes=14 << 20),
    )(normed, *a1, *b1)
    text_emb = pl.pallas_call(
        text_kernel,
        out_shape=jax.ShapeDtypeStruct((PAIRS, D), BF),
        in_specs=[VM] * 3,
        out_specs=VM,
        name="text",
        cost_estimate=pl.CostEstimate(flops=2 * PAIRS * D * D, transcendentals=0, bytes_accessed=5 << 20),
        compiler_params=pltpu.CompilerParams(vmem_limit_bytes=12 << 20),
    )(normaliser_multipliers[2:3], caption_mapping_matrix, texts)
    units, text_emb = lax.optimization_barrier((units, text_emb))
    half_cost = pl.CostEstimate(flops=2 * 1024 * D * HID, transcendentals=0, bytes_accessed=12 << 20)
    sent, second = pl.pallas_call(
        contract_sent_kernel,
        out_shape=(jax.ShapeDtypeStruct((512, D), BF), jax.ShapeDtypeStruct((2, D, HID), BF)),
        in_specs=[VM] * 11,
        out_specs=(VM, VM),
        name="contract_sent",
        cost_estimate=half_cost,
        compiler_params=pltpu.CompilerParams(vmem_limit_bytes=14 << 20),
    )(units, *a2, *b2)
    received = lax.ppermute(sent, "c", [(0, 1), (1, 0)])
    own = pl.pallas_call(
        contract_own_kernel,
        out_shape=jax.ShapeDtypeStruct((512, D), F32),
        in_specs=[VM, VM],
        out_specs=VM,
        name="contract_own",
        cost_estimate=half_cost,
        compiler_params=pltpu.CompilerParams(vmem_limit_bytes=14 << 20),
    )(units, second)
    message = pl.pallas_call(
        last_kernel,
        out_shape=jax.ShapeDtypeStruct((64, 4, 16), F32),
        in_specs=[SM, SM, VM, VM, VM, VM, VM],
        out_specs=VM,
        name="losses",
        compiler_params=pltpu.CompilerParams(vmem_limit_bytes=12 << 20),
    )(sharpness_factor, score_offset_term, own_rows, own, received, normaliser_multipliers[1:2], text_emb)
    arrived = jnp.sum(lax.all_to_all(message.reshape(256, 16), ALL, 0, 0, tiled=True), axis=0)
    return arrived[8:], arrived[:8]


def solution(mesh):
    finer = Mesh(mesh.devices.reshape(4, 2, 8, 2, 2), ALL)
    dp, mp = DP, ("xl", "c")
    in_specs = (P(dp, None), P(dp, None), P(), P(dp, mp), P(mp, dp), P(), P(), P())
    out_specs = (P(dp), P(dp))

    return jax.shard_map(on_device, mesh=finer, in_specs=in_specs, out_specs=out_specs, check_vma=False)
```

profile of v0, /device:TPU:2, one launch (start us, length us, event | category | flops | bytes accessed | tf_op | source)
XLA Modules:
  0.0 145.2 jit_solution(7611477839973693069)
XLA Ops:
  0.7 0.7 copy-done
  1.4 0.9 fusion.2
  2.3 3.3 %collective-permute-start.2 = (bf16[40,1152]{1,0:T(8,128)(2,1)S(1)}, bf16[40,1152]{1,0:T(8,128)(2,1)S(1)}, u32[]{:S(2)}, u32[]{:S(2)}) collective-permute-start(bf16[40,1152]{1,0:T(8,128)(2,1)S(1)} %get-tuple-element.19), channel_id=1, source_target_pairs={{0,8},{4,12},{8,16},{12,20},{16,24},{20,28},{24,0},{28,4},{1,9},{5... | collective-permute-start | bytes 276488 | tf_op jit(solution)/shard_map/ppermute | solution.py:23
  5.7 3.1 %collective-permute-start.3 = (bf16[40,1152]{1,0:T(8,128)(2,1)S(1)}, bf16[40,1152]{1,0:T(8,128)(2,1)S(1)}, u32[]{:S(2)}, u32[]{:S(2)}) collective-permute-start(bf16[40,1152]{1,0:T(8,128)(2,1)S(1)} %get-tuple-element.19), channel_id=1, source_target_pairs={{0,24},{4,28},{8,0},{12,4},{16,8},{20,12},{24,16},{28,20},{1,25},{... | collective-permute-start | bytes 276488 | tf_op jit(solution)/shard_map/ppermute | solution.py:23
  8.8 1.0 collective-permute-start
  9.8 2.2 %collective-permute-start.1 = (bf16[40,1152]{1,0:T(8,128)(2,1)S(1)}, bf16[40,1152]{1,0:T(8,128)(2,1)S(1)}, u32[]{:S(2)}, u32[]{:S(2)}) collective-permute-start(bf16[40,1152]{1,0:T(8,128)(2,1)S(1)} %get-tuple-element.19), channel_id=1, source_target_pairs={{0,28},{4,0},{8,4},{12,8},{16,12},{20,16},{24,20},{28,24},{1,29},{... | collective-permute-start | bytes 276488 | tf_op jit(solution)/shard_map/ppermute | solution.py:23
  12.0 2.9 %collective-permute-start.4 = (bf16[40,1152]{1,0:T(8,128)(2,1)S(1)}, bf16[40,1152]{1,0:T(8,128)(2,1)S(1)}, u32[]{:S(2)}, u32[]{:S(2)}) collective-permute-start(bf16[40,1152]{1,0:T(8,128)(2,1)S(1)} %collective-permute-done.2), channel_id=1, source_target_pairs={{0,4},{4,8},{8,12},{12,16},{16,20},{20,24},{24,28},{28,0},{1,5},{5... | collective-permute-start | bytes 276488 | tf_op jit(solution)/shard_map/ppermute | solution.py:23
  14.9 0.2 collective-permute-done.3
  15.1 2.5 %collective-permute-start.5 = (bf16[40,1152]{1,0:T(8,128)(2,1)S(1)}, bf16[40,1152]{1,0:T(8,128)(2,1)S(1)}, u32[]{:S(2)}, u32[]{:S(2)}) collective-permute-start(bf16[40,1152]{1,0:T(8,128)(2,1)S(1)} %collective-permute-done.3), channel_id=1, source_target_pairs={{0,28},{4,0},{8,4},{12,8},{16,12},{20,16},{24,20},{28,24},{1,29},{... | collective-permute-start | bytes 276488 | tf_op jit(solution)/shard_map/ppermute | solution.py:23
  17.7 1.7 %collective-permute-done.4 = bf16[40,1152]{1,0:T(8,128)(2,1)S(1)} collective-permute-done((bf16[40,1152]{1,0:T(8,128)(2,1)S(1)}, bf16[40,1152]{1,0:T(8,128)(2,1)S(1)}, u32[]{:S(2)}, u32[]{:S(2)}) %collective-permute-start.4) | collective-permute-done | bytes 92192 | tf_op jit(solution)/shard_map/ppermute | solution.py:23
  19.4 2.3 %collective-permute-done.5 = bf16[40,1152]{1,0:T(8,128)(2,1)S(1)} collective-permute-done((bf16[40,1152]{1,0:T(8,128)(2,1)S(1)}, bf16[40,1152]{1,0:T(8,128)(2,1)S(1)}, u32[]{:S(2)}, u32[]{:S(2)}) %collective-permute-start.5) | collective-permute-done | bytes 92192 | tf_op jit(solution)/shard_map/ppermute | solution.py:23
  21.7 0.6 collective-permute-done.6
  22.3 0.1 fusion.4
  22.7 0.1 reshape.17
  22.9 0.6 collective-permute-start.9
  23.5 1.5 %collective-permute-start.7 = (bf16[160,1152]{1,0:T(8,128)(2,1)S(1)}, bf16[160,1152]{1,0:T(8,128)(2,1)S(1)}, u32[]{:S(2)}, u32[]{:S(2)}) collective-permute-start(bf16[160,1152]{1,0:T(8,128)(2,1)S(1)} %pad_maximum_fusion.4), channel_id=1, source_target_pairs={{0,2},{2,32},{32,34},{34,0},{1,3},{3,33},{33,35},{35,1},{4,6},{6,3... | collective-permute-start | bytes 1105928 | tf_op jit(solution)/shard_map/ppermute | solution.py:23
  25.1 3.1 %collective-permute-start.16 = (bf16[160,1152]{1,0:T(8,128)(2,1)S(1)}, bf16[160,1152]{1,0:T(8,128)(2,1)S(1)}, u32[]{:S(2)}, u32[]{:S(2)}) collective-permute-start(bf16[160,1152]{1,0:T(8,128)(2,1)S(1)} %pad_maximum_fusion.5), channel_id=1, source_target_pairs={{0,192},{64,0},{128,64},{192,128},{1,193},{65,1},{129,65},{193,129... | collective-permute-start | bytes 1105928 | tf_op jit(solution)/shard_map/ppermute | solution.py:23
  28.2 4.9 %collective-permute-done.7 = bf16[160,1152]{1,0:T(8,128)(2,1)S(1)} collective-permute-done((bf16[160,1152]{1,0:T(8,128)(2,1)S(1)}, bf16[160,1152]{1,0:T(8,128)(2,1)S(1)}, u32[]{:S(2)}, u32[]{:S(2)}) %collective-permute-start.7) | collective-permute-done | bytes 368672 | tf_op jit(solution)/shard_map/ppermute | solution.py:23
  33.1 0.6 collective-permute-start.8
  33.7 3.7 %collective-permute-done.14 = bf16[160,1152]{1,0:T(8,128)(2,1)S(1)} collective-permute-done((bf16[160,1152]{1,0:T(8,128)(2,1)S(1)}, bf16[160,1152]{1,0:T(8,128)(2,1)S(1)}, u32[]{:S(2)}, u32[]{:S(2)}) %collective-permute-start.14) | collective-permute-done | bytes 368672 | tf_op jit(solution)/shard_map/ppermute | solution.py:23
  37.6 1.6 %collective-permute-start.21 = (bf16[64,1152]{1,0:T(8,128)(2,1)S(1)}, bf16[64,1152]{1,0:T(8,128)(2,1)S(1)}, u32[]{:S(2)}, u32[]{:S(2)}) collective-permute-start(bf16[64,1152]{1,0:T(8,128)(2,1)S(1)} %get-tuple-element.30), channel_id=1, source_target_pairs={{0,34},{2,0},{32,2},{34,32},{1,35},{3,1},{33,3},{35,33},{4,38},{6,... | collective-permute-start | bytes 442376 | tf_op jit(solution)/shard_map/ppermute | solution.py:23
  39.2 3.5 %collective-permute-start.26 = (bf16[80,1152]{1,0:T(8,128)(2,1)S(1)}, bf16[80,1152]{1,0:T(8,128)(2,1)S(1)}, u32[]{:S(2)}, u32[]{:S(2)}) collective-permute-start(bf16[80,1152]{1,0:T(8,128)(2,1)S(1)} %get-tuple-element.27), channel_id=1, source_target_pairs={{0,192},{64,0},{128,64},{192,128},{1,193},{65,1},{129,65},{193,129... | collective-permute-start | bytes 552968 | tf_op jit(solution)/shard_map/ppermute | solution.py:23
  42.7 1.5 %collective-permute-done.15 = bf16[80,1152]{1,0:T(8,128)(2,1)S(1)} collective-permute-done((bf16[80,1152]{1,0:T(8,128)(2,1)S(1)}, bf16[80,1152]{1,0:T(8,128)(2,1)S(1)}, u32[]{:S(2)}, u32[]{:S(2)}) %collective-permute-start.15) | collective-permute-done | bytes 184352 | tf_op jit(solution)/shard_map/ppermute | solution.py:23
  44.3 0.1 pad_maximum_fusion.1.refs_5_
  44.4 1.6 %collective-permute-start.17 = (bf16[4,80,1152]{2,1,0:T(8,128)(2,1)S(1)}, bf16[4,80,1152]{2,1,0:T(8,128)(2,1)S(1)}, u32[]{:S(2)}, u32[]{:S(2)}) collective-permute-start(bf16[4,80,1152]{2,1,0:T(8,128)(2,1)S(1)} %pad_maximum_fusion.1.refs_5_), channel_id=1, source_target_pairs={{0,2},{2,32},{32,34},{34,0},{1,3},{3,33},{33,35},{35,1},{4,6},{6,3... | collective-permute-start | bytes 2211848 | tf_op jit(solution)/shard_map/ppermute | solution.py:23
  45.9 0.5 collective-permute-start.18
  46.5 0.1 pad_maximum_fusion.refs_0_
  46.7 3.3 %collective-permute-start.11 = (bf16[4,96,1152]{2,1,0:T(8,128)(2,1)S(1)}, bf16[4,96,1152]{2,1,0:T(8,128)(2,1)S(1)}, u32[]{:S(2)}, u32[]{:S(2)}) collective-permute-start(bf16[4,96,1152]{2,1,0:T(8,128)(2,1)S(1)} %pad_maximum_fusion.refs_0_), channel_id=1, source_target_pairs={{0,192},{64,0},{128,64},{192,128},{1,193},{65,1},{129,65},{193,129... | collective-permute-start | bytes 2654216 | tf_op jit(solution)/shard_map/ppermute | solution.py:23
  50.0 0.1 pad_maximum_fusion.2.refs_5_
  50.2 2.0 %collective-permute-start.27 = (bf16[4,80,1152]{2,1,0:T(8,128)(2,1)S(1)}, bf16[4,80,1152]{2,1,0:T(8,128)(2,1)S(1)}, u32[]{:S(2)}, u32[]{:S(2)}) collective-permute-start(bf16[4,80,1152]{2,1,0:T(8,128)(2,1)S(1)} %pad_maximum_fusion.2.refs_5_), channel_id=1, source_target_pairs={{0,2},{2,32},{32,34},{34,0},{1,3},{3,33},{33,35},{35,1},{4,6},{6,3... | collective-permute-start | bytes 2211848 | tf_op jit(solution)/shard_map/ppermute | solution.py:23
  52.2 11.6 %collective-permute-done.17.refs_6_ = bf16[4,80,1152]{2,1,0:T(8,128)(2,1)S(1)} collective-permute-done((bf16[4,80,1152]{2,1,0:T(8,128)(2,1)S(1)}, bf16[4,80,1152]{2,1,0:T(8,128)(2,1)S(1)}, u32[]{:S(2)}, u32[]{:S(2)}) %collective-permute-start.17) | collective-permute-done | bytes 737312 | tf_op jit(solution)/shard_map/ppermute | solution.py:23
  63.8 3.2 %collective-permute-start.23 = (bf16[4,64,1152]{2,1,0:T(8,128)(2,1)S(1)}, bf16[4,64,1152]{2,1,0:T(8,128)(2,1)S(1)}, u32[]{:S(2)}, u32[]{:S(2)}) collective-permute-start(bf16[4,64,1152]{2,1,0:T(8,128)(2,1)S(1)} %pad_maximum_fusion.3.refs_0_), channel_id=1, source_target_pairs={{0,192},{64,0},{128,64},{192,128},{1,193},{65,1},{129,65},{193,129... | collective-permute-start | bytes 1769480 | tf_op jit(solution)/shard_map/ppermute | solution.py:23
  67.1 3.4 %collective-permute-done.10.refs_1_ = bf16[4,96,1152]{2,1,0:T(8,128)(2,1)S(1)} collective-permute-done((bf16[4,96,1152]{2,1,0:T(8,128)(2,1)S(1)}, bf16[4,96,1152]{2,1,0:T(8,128)(2,1)S(1)}, u32[]{:S(2)}, u32[]{:S(2)}) %collective-permute-start.10) | collective-permute-done | bytes 884768 | tf_op jit(solution)/shard_map/ppermute | solution.py:23
  70.4 2.8 %collective-permute-start.28 = (bf16[4,80,1152]{2,1,0:T(8,128)(2,1)S(1)}, bf16[4,80,1152]{2,1,0:T(8,128)(2,1)S(1)}, u32[]{:S(2)}, u32[]{:S(2)}) collective-permute-start(bf16[4,80,1152]{2,1,0:T(8,128)(2,1)S(1)} %pad_maximum_fusion.2.refs_5_), channel_id=1, source_target_pairs={{0,34},{2,0},{32,2},{34,32},{1,35},{3,1},{33,3},{35,33},{4,38},{6,... | collective-permute-start | bytes 2211848 | tf_op jit(solution)/shard_map/ppermute | solution.py:23
  73.5 4.1 %collective-permute-done.22.refs_1_ = bf16[4,64,1152]{2,1,0:T(8,128)(2,1)S(1)} collective-permute-done((bf16[4,64,1152]{2,1,0:T(8,128)(2,1)S(1)}, bf16[4,64,1152]{2,1,0:T(8,128)(2,1)S(1)}, u32[]{:S(2)}, u32[]{:S(2)}) %collective-permute-start.22) | collective-permute-done | bytes 589856 | tf_op jit(solution)/shard_map/ppermute | solution.py:23
  77.5 3.6 %collective-permute-start.20 = (bf16[2,80,1152]{2,1,0:T(8,128)(2,1)S(1)}, bf16[2,80,1152]{2,1,0:T(8,128)(2,1)S(1)}, u32[]{:S(2)}, u32[]{:S(2)}) collective-permute-start(bf16[2,80,1152]{2,1,0:T(8,128)(2,1)S(1)} %slice.150), channel_id=1, source_target_pairs={{0,34},{2,0},{32,2},{34,32},{1,35},{3,1},{33,3},{35,33},{4,38},{6,... | collective-permute-start | bytes 1105928 | tf_op jit(solution)/shard_map/ppermute | solution.py:23
  81.2 3.2 %collective-permute-start.13 = (bf16[2,96,1152]{2,1,0:T(8,128)(2,1)S(1)}, bf16[2,96,1152]{2,1,0:T(8,128)(2,1)S(1)}, u32[]{:S(2)}, u32[]{:S(2)}) collective-permute-start(bf16[2,96,1152]{2,1,0:T(8,128)(2,1)S(1)} %slice.143), channel_id=1, source_target_pairs={{0,192},{64,0},{128,64},{192,128},{1,193},{65,1},{129,65},{193,129... | collective-permute-start | bytes 1327112 | tf_op jit(solution)/shard_map/ppermute | solution.py:23
  84.4 6.7 %norm.1 = (bf16[1024,1152]{1,0:T(8,128)(2,1)S(1)}, bf16[512,1152]{1,0:T(8,128)(2,1)S(1)}) custom-call(bf16[2048,1152]{1,0:T(8,128)(2,1)S(1)} %bitcast.49, f32[1,1152]{1,0:T(1,128)S(1)} %get-tuple-element.39.gain_ref), custom_call_target="tpu_custom_call" | custom-call | flops 23592960 | bytes 6291456 | tf_op jit(solution)/shard_map/norm/pallas_call | solution.py:265
  91.4 3.3 %collective-permute-start.25 = (bf16[2,64,1152]{2,1,0:T(8,128)(2,1)S(1)}, bf16[2,64,1152]{2,1,0:T(8,128)(2,1)S(1)}, u32[]{:S(2)}, u32[]{:S(2)}) collective-permute-start(bf16[2,64,1152]{2,1,0:T(8,128)(2,1)S(1)} %slice.154), channel_id=1, source_target_pairs={{0,192},{64,0},{128,64},{192,128},{1,193},{65,1},{129,65},{193,129... | collective-permute-start | bytes 884744 | tf_op jit(solution)/shard_map/ppermute | solution.py:23
  94.7 2.0 %collective-permute-start.30 = (bf16[2,80,1152]{2,1,0:T(8,128)(2,1)S(1)}, bf16[2,80,1152]{2,1,0:T(8,128)(2,1)S(1)}, u32[]{:S(2)}, u32[]{:S(2)}) collective-permute-start(bf16[2,80,1152]{2,1,0:T(8,128)(2,1)S(1)} %slice.158), channel_id=1, source_target_pairs={{0,34},{2,0},{32,2},{34,32},{1,35},{3,1},{33,3},{35,33},{4,38},{6,... | collective-permute-start | bytes 1105928 | tf_op jit(solution)/shard_map/ppermute | solution.py:23
  96.7 8.2 %widen.1 = (bf16[2,1024,1152]{2,1,0:T(8,128)(2,1)S(1)}, bf16[512,1152]{1,0:T(8,128)(2,1)S(1)}) custom-call(bf16[1024,1152]{1,0:T(8,128)(2,1)S(1)} %get-tuple-element.11.normed_ref, bf16[4,96,1152]{2,1,0:T(8,128)(2,1)S(1)} %pad_maximum_fusion.refs_0_, bf16[4,96,1152]{2,1,0:T(8,128)(2,1)S(1)} %collective-permute-done.10.refs_1_, ...), custom_call_target="tpu_custom_call" | custom-call | flops 5435817984 | bytes 12582912 | tf_op jit(solution)/shard_map/widen/pallas_call | solution.py:277
  104.9 3.7 %text.1.text_ref = bf16[512,1152]{1,0:T(8,128)(2,1)S(1)} custom-call(f32[1,1152]{1,0:T(1,128)S(1)} %get-tuple-element.40.gain_ref, bf16[1152,1152]{1,0:T(8,128)(2,1)S(1)} %copy-done.1, bf16[512,1152]{1,0:T(8,128)(2,1)S(1)} %get-tuple-element.13.rows_ref), custom_call_target="tpu_custom_call" | custom-call | flops 1358954496 | bytes 5242880 | tf_op jit(solution)/shard_map/text/pallas_call | solution.py:287
  108.6 4.3 %contract_sent.1 = (bf16[512,1152]{1,0:T(8,128)(2,1)S(1)}, bf16[2,1152,1152]{2,1,0:T(8,128)(2,1)S(1)}) custom-call(bf16[2,1024,1152]{2,1,0:T(8,128)(2,1)S(1)} %get-tuple-element.14.h, bf16[4,64,1152]{2,1,0:T(8,128)(2,1)S(1)} %pad_maximum_fusion.3.refs_0_, bf16[4,64,1152]{2,1,0:T(8,128)(2,1)S(1)} %collective-permute-done.22.refs_1_, ...), custom_call_target="tpu_custom_call" | custom-call | flops 2717908992 | bytes 12582912 | tf_op jit(solution)/shard_map/contract_sent/pallas_call | solution.py:298
  114.3 3.8 %contract_own.1.own_ref = f32[512,1152]{1,0:T(8,128)S(1)} custom-call(bf16[2,1024,1152]{2,1,0:T(8,128)(2,1)S(1)} %get-tuple-element.14.h, bf16[2,1152,1152]{2,1,0:T(8,128)(2,1)S(1)} %get-tuple-element.15.w2), custom_call_target="tpu_custom_call" | custom-call | flops 2717908992 | bytes 12582912 | tf_op jit(solution)/shard_map/contract_own/pallas_call | solution.py:308
  118.1 3.1 %losses.1 = f32[64,4,16]{2,1,0:T(4,128)S(1)} custom-call(f32[1]{0:T(128)S(6)} %copy.19.scale_ref, f32[1]{0:T(128)S(6)} %copy.20.shift_ref, bf16[512,1152]{1,0:T(8,128)(2,1)S(1)} %get-tuple-element.10.x_ref, f32[512,1152]{1,0:T(8,128)S(1)} %contract_own.1.own_ref, bf16[512,1152]{1,0:T(8,128)(2,1)S(1)} %collective-permute-done.31.recv_ref, ...), custom_call_target="tpu_custom_call" | custom-call | tf_op jit(solution)/shard_map/losses/pallas_call | solution.py:317
  121.3 23.0 %all_to_all.9 = f32[256,1,16]{2,1,0:T(1,128)S(1)} all-to-all(f32[256,1,16]{2,1,0:T(1,128)S(1)} %bitcast.50), channel_id=1, replica_groups=mesh['y'=4,'xh'=2,'z'=8,'xl'=2,'c'=2] {'y','xh','z','xl','c'}, dimensions={0} | all-to-all | bytes 32768 | tf_op jit(solution)/shard_map/all_to_all | solution.py:325
  144.3 0.3 reduce_sum.9
  144.6 0.6 fusion.8
  (80 shorter events, 1.6 us)
Async XLA Ops:
  0.6 0.7 copy-start
  2.3 9.7 %collective-permute-start.2 = (bf16[40,1152]{1,0:T(8,128)(2,1)S(1)}, bf16[40,1152]{1,0:T(8,128)(2,1)S(1)}, u32[]{:S(2)}, u32[]{:S(2)}) collective-permute-start(bf16[40,1152]{1,0:T(8,128)(2,1)S(1)} %get-tuple-element.19), channel_id=1, source_target_pairs={{0,8},{4,12},{8,16},{12,20},{16,24},{20,28},{24,0},{28,4},{1,9},{5... | collective-permute-start | bytes 276488 | tf_op jit(solution)/shard_map/ppermute | solution.py:23
  5.7 9.4 %collective-permute-start.3 = (bf16[40,1152]{1,0:T(8,128)(2,1)S(1)}, bf16[40,1152]{1,0:T(8,128)(2,1)S(1)}, u32[]{:S(2)}, u32[]{:S(2)}) collective-permute-start(bf16[40,1152]{1,0:T(8,128)(2,1)S(1)} %get-tuple-element.19), channel_id=1, source_target_pairs={{0,24},{4,28},{8,0},{12,4},{16,8},{20,12},{24,16},{28,20},{1,25},{... | collective-permute-start | bytes 276488 | tf_op jit(solution)/shard_map/ppermute | solution.py:23
  8.8 8.8 %collective-permute-start = (bf16[40,1152]{1,0:T(8,128)(2,1)S(1)}, bf16[40,1152]{1,0:T(8,128)(2,1)S(1)}, u32[]{:S(2)}, u32[]{:S(2)}) collective-permute-start(bf16[40,1152]{1,0:T(8,128)(2,1)S(1)} %get-tuple-element.19), channel_id=1, source_target_pairs={{0,4},{4,8},{8,12},{12,16},{16,20},{20,24},{24,28},{28,0},{1,5},{5... | collective-permute-start | bytes 276488 | tf_op jit(solution)/shard_map/ppermute | solution.py:23
  9.8 7.8 %collective-permute-start.1 = (bf16[40,1152]{1,0:T(8,128)(2,1)S(1)}, bf16[40,1152]{1,0:T(8,128)(2,1)S(1)}, u32[]{:S(2)}, u32[]{:S(2)}) collective-permute-start(bf16[40,1152]{1,0:T(8,128)(2,1)S(1)} %get-tuple-element.19), channel_id=1, source_target_pairs={{0,28},{4,0},{8,4},{12,8},{16,12},{20,16},{24,20},{28,24},{1,29},{... | collective-permute-start | bytes 276488 | tf_op jit(solution)/shard_map/ppermute | solution.py:23
  12.0 7.3 %collective-permute-start.4 = (bf16[40,1152]{1,0:T(8,128)(2,1)S(1)}, bf16[40,1152]{1,0:T(8,128)(2,1)S(1)}, u32[]{:S(2)}, u32[]{:S(2)}) collective-permute-start(bf16[40,1152]{1,0:T(8,128)(2,1)S(1)} %collective-permute-done.2), channel_id=1, source_target_pairs={{0,4},{4,8},{8,12},{12,16},{16,20},{20,24},{24,28},{28,0},{1,5},{5... | collective-permute-start | bytes 276488 | tf_op jit(solution)/shard_map/ppermute | solution.py:23
  14.9 7.4 %collective-permute-start.6 = (bf16[40,1152]{1,0:T(8,128)(2,1)S(1)}, bf16[40,1152]{1,0:T(8,128)(2,1)S(1)}, u32[]{:S(2)}, u32[]{:S(2)}) collective-permute-start(bf16[40,1152]{1,0:T(8,128)(2,1)S(1)} %collective-permute-done.2), channel_id=1, source_target_pairs={{0,8},{4,12},{8,16},{12,20},{16,24},{20,28},{24,0},{28,4},{1,9},{5... | collective-permute-start | bytes 276488 | tf_op jit(solution)/shard_map/ppermute | solution.py:23
  15.1 6.6 %collective-permute-start.5 = (bf16[40,1152]{1,0:T(8,128)(2,1)S(1)}, bf16[40,1152]{1,0:T(8,128)(2,1)S(1)}, u32[]{:S(2)}, u32[]{:S(2)}) collective-permute-start(bf16[40,1152]{1,0:T(8,128)(2,1)S(1)} %collective-permute-done.3), channel_id=1, source_target_pairs={{0,28},{4,0},{8,4},{12,8},{16,12},{20,16},{24,20},{28,24},{1,29},{... | collective-permute-start | bytes 276488 | tf_op jit(solution)/shard_map/ppermute | solution.py:23
  22.9 14.7 %collective-permute-start.9 = (bf16[160,1152]{1,0:T(8,128)(2,1)S(1)}, bf16[160,1152]{1,0:T(8,128)(2,1)S(1)}, u32[]{:S(2)}, u32[]{:S(2)}) collective-permute-start(bf16[160,1152]{1,0:T(8,128)(2,1)S(1)} %pad_maximum_fusion.4), channel_id=1, source_target_pairs={{0,34},{2,0},{32,2},{34,32},{1,35},{3,1},{33,3},{35,33},{4,38},{6,... | collective-permute-start | bytes 1105928 | tf_op jit(solution)/shard_map/ppermute | solution.py:23
  23.5 9.6 %collective-permute-start.7 = (bf16[160,1152]{1,0:T(8,128)(2,1)S(1)}, bf16[160,1152]{1,0:T(8,128)(2,1)S(1)}, u32[]{:S(2)}, u32[]{:S(2)}) collective-permute-start(bf16[160,1152]{1,0:T(8,128)(2,1)S(1)} %pad_maximum_fusion.4), channel_id=1, source_target_pairs={{0,2},{2,32},{32,34},{34,0},{1,3},{3,33},{33,35},{35,1},{4,6},{6,3... | collective-permute-start | bytes 1105928 | tf_op jit(solution)/shard_map/ppermute | solution.py:23
  25.1 14.1 %collective-permute-start.16 = (bf16[160,1152]{1,0:T(8,128)(2,1)S(1)}, bf16[160,1152]{1,0:T(8,128)(2,1)S(1)}, u32[]{:S(2)}, u32[]{:S(2)}) collective-permute-start(bf16[160,1152]{1,0:T(8,128)(2,1)S(1)} %pad_maximum_fusion.5), channel_id=1, source_target_pairs={{0,192},{64,0},{128,64},{192,128},{1,193},{65,1},{129,65},{193,129... | collective-permute-start | bytes 1105928 | tf_op jit(solution)/shard_map/ppermute | solution.py:23
  28.2 9.2 %collective-permute-start.14 = (bf16[160,1152]{1,0:T(8,128)(2,1)S(1)}, bf16[160,1152]{1,0:T(8,128)(2,1)S(1)}, u32[]{:S(2)}, u32[]{:S(2)}) collective-permute-start(bf16[160,1152]{1,0:T(8,128)(2,1)S(1)} %pad_maximum_fusion.5), channel_id=1, source_target_pairs={{0,64},{64,128},{128,192},{192,0},{1,65},{65,129},{129,193},{193,1... | collective-permute-start | bytes 1105928 | tf_op jit(solution)/shard_map/ppermute | solution.py:23
  33.1 51.3 %slice-start = ((s8[4718592]{0:T(1024)(128)(4,1)}), s8[4194304]{0:T(1024)(128)(4,1)S(1)}, s32[]{:S(2)}) async-start(s8[4718592]{0:T(1024)(128)(4,1)} %bitcast.48), calls=%async_computation.1 | async-start | bytes 8388608
  33.1 13.4 %collective-permute-start.8 = (bf16[96,1152]{1,0:T(8,128)(2,1)S(1)}, bf16[96,1152]{1,0:T(8,128)(2,1)S(1)}, u32[]{:S(2)}, u32[]{:S(2)}) collective-permute-start(bf16[96,1152]{1,0:T(8,128)(2,1)S(1)} %get-tuple-element.33), channel_id=1, source_target_pairs={{0,2},{2,32},{32,34},{34,0},{1,3},{3,33},{33,35},{35,1},{4,6},{6,3... | collective-permute-start | bytes 663560 | tf_op jit(solution)/shard_map/ppermute | solution.py:23
  37.4 6.8 %collective-permute-start.15 = (bf16[80,1152]{1,0:T(8,128)(2,1)S(1)}, bf16[80,1152]{1,0:T(8,128)(2,1)S(1)}, u32[]{:S(2)}, u32[]{:S(2)}) collective-permute-start(bf16[80,1152]{1,0:T(8,128)(2,1)S(1)} %get-tuple-element.26), channel_id=1, source_target_pairs={{0,64},{64,128},{128,192},{192,0},{1,65},{65,129},{129,193},{193,1... | collective-permute-start | bytes 552968 | tf_op jit(solution)/shard_map/ppermute | solution.py:23
  37.6 12.6 %collective-permute-start.21 = (bf16[64,1152]{1,0:T(8,128)(2,1)S(1)}, bf16[64,1152]{1,0:T(8,128)(2,1)S(1)}, u32[]{:S(2)}, u32[]{:S(2)}) collective-permute-start(bf16[64,1152]{1,0:T(8,128)(2,1)S(1)} %get-tuple-element.30), channel_id=1, source_target_pairs={{0,34},{2,0},{32,2},{34,32},{1,35},{3,1},{33,3},{35,33},{4,38},{6,... | collective-permute-start | bytes 442376 | tf_op jit(solution)/shard_map/ppermute | solution.py:23
  39.2 7.5 %collective-permute-start.26 = (bf16[80,1152]{1,0:T(8,128)(2,1)S(1)}, bf16[80,1152]{1,0:T(8,128)(2,1)S(1)}, u32[]{:S(2)}, u32[]{:S(2)}) collective-permute-start(bf16[80,1152]{1,0:T(8,128)(2,1)S(1)} %get-tuple-element.27), channel_id=1, source_target_pairs={{0,192},{64,0},{128,64},{192,128},{1,193},{65,1},{129,65},{193,129... | collective-permute-start | bytes 552968 | tf_op jit(solution)/shard_map/ppermute | solution.py:23
  44.4 19.4 %collective-permute-start.17 = (bf16[4,80,1152]{2,1,0:T(8,128)(2,1)S(1)}, bf16[4,80,1152]{2,1,0:T(8,128)(2,1)S(1)}, u32[]{:S(2)}, u32[]{:S(2)}) collective-permute-start(bf16[4,80,1152]{2,1,0:T(8,128)(2,1)S(1)} %pad_maximum_fusion.1.refs_5_), channel_id=1, source_target_pairs={{0,2},{2,32},{32,34},{34,0},{1,3},{3,33},{33,35},{35,1},{4,6},{6,3... | collective-permute-start | bytes 2211848 | tf_op jit(solution)/shard_map/ppermute | solution.py:23
  45.9 17.9 %collective-permute-start.18 = (bf16[4,80,1152]{2,1,0:T(8,128)(2,1)S(1)}, bf16[4,80,1152]{2,1,0:T(8,128)(2,1)S(1)}, u32[]{:S(2)}, u32[]{:S(2)}) collective-permute-start(bf16[4,80,1152]{2,1,0:T(8,128)(2,1)S(1)} %pad_maximum_fusion.1.refs_5_), channel_id=1, source_target_pairs={{0,34},{2,0},{32,2},{34,32},{1,35},{3,1},{33,3},{35,33},{4,38},{6,... | collective-permute-start | bytes 2211848 | tf_op jit(solution)/shard_map/ppermute | solution.py:23
  46.5 37.9 %slice-start.1 = ((s8[4718592]{0:T(1024)(128)(4,1)}), s8[524288]{0:T(1024)(128)(4,1)S(1)}, s32[]{:S(2)}) async-start(s8[4718592]{0:T(1024)(128)(4,1)} %bitcast.48), calls=%async_computation.2 | async-start | bytes 1048576
  46.6 23.8 %collective-permute-start.10 = (bf16[4,96,1152]{2,1,0:T(8,128)(2,1)S(1)}, bf16[4,96,1152]{2,1,0:T(8,128)(2,1)S(1)}, u32[]{:S(2)}, u32[]{:S(2)}) collective-permute-start(bf16[4,96,1152]{2,1,0:T(8,128)(2,1)S(1)} %pad_maximum_fusion.refs_0_), channel_id=1, source_target_pairs={{0,64},{64,128},{128,192},{192,0},{1,65},{65,129},{129,193},{193,1... | collective-permute-start | bytes 2654216 | tf_op jit(solution)/shard_map/ppermute | solution.py:23
  46.7 26.6 %collective-permute-start.11 = (bf16[4,96,1152]{2,1,0:T(8,128)(2,1)S(1)}, bf16[4,96,1152]{2,1,0:T(8,128)(2,1)S(1)}, u32[]{:S(2)}, u32[]{:S(2)}) collective-permute-start(bf16[4,96,1152]{2,1,0:T(8,128)(2,1)S(1)} %pad_maximum_fusion.refs_0_), channel_id=1, source_target_pairs={{0,192},{64,0},{128,64},{192,128},{1,193},{65,1},{129,65},{193,129... | collective-permute-start | bytes 2654216 | tf_op jit(solution)/shard_map/ppermute | solution.py:23
  50.2 34.2 %copy-start.2 = (f32[3,1152]{1,0:T(4,128)S(1)}, f32[3,1152]{1,0:T(4,128)}, u32[]{:S(2)}) copy-start(f32[3,1152]{1,0:T(4,128)} %param.10) | copy-start | bytes 41476
  50.2 31.0 %collective-permute-start.27 = (bf16[4,80,1152]{2,1,0:T(8,128)(2,1)S(1)}, bf16[4,80,1152]{2,1,0:T(8,128)(2,1)S(1)}, u32[]{:S(2)}, u32[]{:S(2)}) collective-permute-start(bf16[4,80,1152]{2,1,0:T(8,128)(2,1)S(1)} %pad_maximum_fusion.2.refs_5_), channel_id=1, source_target_pairs={{0,2},{2,32},{32,34},{34,0},{1,3},{3,33},{33,35},{35,1},{4,6},{6,3... | collective-permute-start | bytes 2211848 | tf_op jit(solution)/shard_map/ppermute | solution.py:23
  63.8 13.7 %collective-permute-start.22 = (bf16[4,64,1152]{2,1,0:T(8,128)(2,1)S(1)}, bf16[4,64,1152]{2,1,0:T(8,128)(2,1)S(1)}, u32[]{:S(2)}, u32[]{:S(2)}) collective-permute-start(bf16[4,64,1152]{2,1,0:T(8,128)(2,1)S(1)} %pad_maximum_fusion.3.refs_0_), channel_id=1, source_target_pairs={{0,64},{64,128},{128,192},{192,0},{1,65},{65,129},{129,193},{193,1... | collective-permute-start | bytes 1769480 | tf_op jit(solution)/shard_map/ppermute | solution.py:23
  63.8 17.3 %collective-permute-start.23 = (bf16[4,64,1152]{2,1,0:T(8,128)(2,1)S(1)}, bf16[4,64,1152]{2,1,0:T(8,128)(2,1)S(1)}, u32[]{:S(2)}, u32[]{:S(2)}) collective-permute-start(bf16[4,64,1152]{2,1,0:T(8,128)(2,1)S(1)} %pad_maximum_fusion.3.refs_0_), channel_id=1, source_target_pairs={{0,192},{64,0},{128,64},{192,128},{1,193},{65,1},{129,65},{193,129... | collective-permute-start | bytes 1769480 | tf_op jit(solution)/shard_map/ppermute | solution.py:23
  70.4 20.8 %collective-permute-start.28 = (bf16[4,80,1152]{2,1,0:T(8,128)(2,1)S(1)}, bf16[4,80,1152]{2,1,0:T(8,128)(2,1)S(1)}, u32[]{:S(2)}, u32[]{:S(2)}) collective-permute-start(bf16[4,80,1152]{2,1,0:T(8,128)(2,1)S(1)} %pad_maximum_fusion.2.refs_5_), channel_id=1, source_target_pairs={{0,34},{2,0},{32,2},{34,32},{1,35},{3,1},{33,3},{35,33},{4,38},{6,... | collective-permute-start | bytes 2211848 | tf_op jit(solution)/shard_map/ppermute | solution.py:23
  73.3 18.0 %collective-permute-start.19 = (bf16[2,80,1152]{2,1,0:T(8,128)(2,1)S(1)}, bf16[2,80,1152]{2,1,0:T(8,128)(2,1)S(1)}, u32[]{:S(2)}, u32[]{:S(2)}) collective-permute-start(bf16[2,80,1152]{2,1,0:T(8,128)(2,1)S(1)} %slice.149), channel_id=1, source_target_pairs={{0,2},{2,32},{32,34},{34,0},{1,3},{3,33},{33,35},{35,1},{4,6},{6,3... | collective-permute-start | bytes 1105928 | tf_op jit(solution)/shard_map/ppermute | solution.py:23
  77.5 17.1 %collective-permute-start.20 = (bf16[2,80,1152]{2,1,0:T(8,128)(2,1)S(1)}, bf16[2,80,1152]{2,1,0:T(8,128)(2,1)S(1)}, u32[]{:S(2)}, u32[]{:S(2)}) collective-permute-start(bf16[2,80,1152]{2,1,0:T(8,128)(2,1)S(1)} %slice.150), channel_id=1, source_target_pairs={{0,34},{2,0},{32,2},{34,32},{1,35},{3,1},{33,3},{35,33},{4,38},{6,... | collective-permute-start | bytes 1105928 | tf_op jit(solution)/shard_map/ppermute | solution.py:23
  81.2 13.5 %collective-permute-start.12 = (bf16[2,96,1152]{2,1,0:T(8,128)(2,1)S(1)}, bf16[2,96,1152]{2,1,0:T(8,128)(2,1)S(1)}, u32[]{:S(2)}, u32[]{:S(2)}) collective-permute-start(bf16[2,96,1152]{2,1,0:T(8,128)(2,1)S(1)} %slice.142), channel_id=1, source_target_pairs={{0,64},{64,128},{128,192},{192,0},{1,65},{65,129},{129,193},{193,1... | collective-permute-start | bytes 1327112 | tf_op jit(solution)/shard_map/ppermute | solution.py:23
  81.2 15.5 %collective-permute-start.13 = (bf16[2,96,1152]{2,1,0:T(8,128)(2,1)S(1)}, bf16[2,96,1152]{2,1,0:T(8,128)(2,1)S(1)}, u32[]{:S(2)}, u32[]{:S(2)}) collective-permute-start(bf16[2,96,1152]{2,1,0:T(8,128)(2,1)S(1)} %slice.143), channel_id=1, source_target_pairs={{0,192},{64,0},{128,64},{192,128},{1,193},{65,1},{129,65},{193,129... | collective-permute-start | bytes 1327112 | tf_op jit(solution)/shard_map/ppermute | solution.py:23
  91.2 17.3 %collective-permute-start.24 = (bf16[2,64,1152]{2,1,0:T(8,128)(2,1)S(1)}, bf16[2,64,1152]{2,1,0:T(8,128)(2,1)S(1)}, u32[]{:S(2)}, u32[]{:S(2)}) collective-permute-start(bf16[2,64,1152]{2,1,0:T(8,128)(2,1)S(1)} %slice.153), channel_id=1, source_target_pairs={{0,64},{64,128},{128,192},{192,0},{1,65},{65,129},{129,193},{193,1... | collective-permute-start | bytes 884744 | tf_op jit(solution)/shard_map/ppermute | solution.py:23
  91.4 17.2 %collective-permute-start.25 = (bf16[2,64,1152]{2,1,0:T(8,128)(2,1)S(1)}, bf16[2,64,1152]{2,1,0:T(8,128)(2,1)S(1)}, u32[]{:S(2)}, u32[]{:S(2)}) collective-permute-start(bf16[2,64,1152]{2,1,0:T(8,128)(2,1)S(1)} %slice.154), channel_id=1, source_target_pairs={{0,192},{64,0},{128,64},{192,128},{1,193},{65,1},{129,65},{193,129... | collective-permute-start | bytes 884744 | tf_op jit(solution)/shard_map/ppermute | solution.py:23
  94.7 13.9 %collective-permute-start.29 = (bf16[2,80,1152]{2,1,0:T(8,128)(2,1)S(1)}, bf16[2,80,1152]{2,1,0:T(8,128)(2,1)S(1)}, u32[]{:S(2)}, u32[]{:S(2)}) collective-permute-start(bf16[2,80,1152]{2,1,0:T(8,128)(2,1)S(1)} %slice.157), channel_id=1, source_target_pairs={{0,2},{2,32},{32,34},{34,0},{1,3},{3,33},{33,35},{35,1},{4,6},{6,3... | collective-permute-start | bytes 1105928 | tf_op jit(solution)/shard_map/ppermute | solution.py:23
  94.7 13.9 %collective-permute-start.30 = (bf16[2,80,1152]{2,1,0:T(8,128)(2,1)S(1)}, bf16[2,80,1152]{2,1,0:T(8,128)(2,1)S(1)}, u32[]{:S(2)}, u32[]{:S(2)}) collective-permute-start(bf16[2,80,1152]{2,1,0:T(8,128)(2,1)S(1)} %slice.158), channel_id=1, source_target_pairs={{0,34},{2,0},{32,2},{34,32},{1,35},{3,1},{33,3},{35,33},{4,38},{6,... | collective-permute-start | bytes 1105928 | tf_op jit(solution)/shard_map/ppermute | solution.py:23
  96.7 8.2 %copy-start.1 = (bf16[1152,1152]{1,0:T(8,128)(2,1)S(1)}, bf16[1152,1152]{1,0:T(8,128)(2,1)}, u32[]{:S(2)}) copy-start(bf16[1152,1152]{1,0:T(8,128)(2,1)} %map_ref.1) | copy-start | bytes 7962628
  112.9 5.2 %collective-permute-start.31 = (bf16[512,1152]{1,0:T(8,128)(2,1)S(1)}, bf16[512,1152]{1,0:T(8,128)(2,1)S(1)}, u32[]{:S(2)}, u32[]{:S(2)}) collective-permute-start(bf16[512,1152]{1,0:T(8,128)(2,1)S(1)} %get-tuple-element.16), channel_id=1, source_target_pairs={{0,1},{1,0},{2,3},{3,2},{4,5},{5,4},{6,7},{7,6},{8,9},{9,8},{10,11... | collective-permute-start | bytes 3538952 | tf_op jit(solution)/shard_map/ppermute | solution.py:307
where the time goes:
time: 147 us; the launch traced here: 145 us
  starting transfers between devices  51.9 us (35%)
  waiting for transfers between devices  34 us (23%)
  Pallas kernels  29.7 us (20%)
  blocking collectives  23 us (16%)
  between operations  2.43 us (2%)
  local copies, waits for them, and re-layouts  2.39 us (2%)
  other arithmetic  1.74 us (1%)
    ppermute x31, starting transfers between devices, shifted(): lax.ppermute(array, axes, [(i, (i + by) % size) for i in range(size)])  51.8 us
    ppermute x31, waiting for transfers between devices, shifted(): lax.ppermute(array, axes, [(i, (i + by) % size) for i in range(size)])  34 us
    all_to_all x1, blocking collectives, on_device(): lax.all_to_all(message.reshape(256, 16), ALL, 0, 0, tiled=True)  23 us
    pallas_call x1, Pallas kernels, on_device(): pl.pallas_call(widen_kernel, out_shape=(jax.ShapeDtypeStruct((2, 1024, HI...  8.18 us
    pallas_call x1, Pallas kernels, on_device(): pl.pallas_call(norm_kernel, out_shape=(jax.ShapeDtypeStruct((1024, D), BF...  6.67 us
    pallas_call x1, Pallas kernels, on_device(): pl.pallas_call(contract_sent_kernel, out_shape=(jax.ShapeDtypeStruct((512...  4.31 us
    pallas_call x1, Pallas kernels, on_device(): pl.pallas_call(contract_own_kernel, out_shape=jax.ShapeDtypeStruct((512,...  3.79 us
    pallas_call x1, Pallas kernels, on_device(): pl.pallas_call(text_kernel, out_shape=jax.ShapeDtypeStruct((PAIRS, D), BF...  3.65 us
  transfers between devices with their start and end apart: 32, of which 10 were waited for; matrix products, arithmetic and copies ran while one was open for 1% of the time, Pallas kernels for 15%

commit v1 on v0

--- a/solution.py
+++ b/solution.py
@@ -14,7 +14,7 @@
 DP = ("y", "xh", "z")
 XS = ("xh", "xl")
 ALL = ("y", "xh", "z", "xl", "c")
-W1A, W1B, W2A, W2B, TX = 80, 64, 64, 80, 16
+W1A, W1B, W2A, W2B, TX = 80, 64, 64, 80, 8
 BF = jnp.bfloat16
 F32 = jnp.float32
 
@@ -99,26 +99,24 @@
     return (0.5 * v * (1.0 + jnp.tanh(inner))).astype(BF)
 
 
-def norm_kernel(x_ref, gain_ref, normed_ref, own_ref, sem):
+def norm_kernel(x_ref, gain_ref, normed_ref, own_ref):
     first = pl.multiple_of(lax.axis_index("xl") * 1024, 1024)
-    copy = pltpu.make_async_copy(x_ref.at[pl.ds(first, 1024), :], normed_ref, sem)
-    copy.start()
-    copy.wait()
-    half = pl.multiple_of(lax.axis_index("c") * 512, 512)
+    half = pl.multiple_of(first + lax.axis_index("c") * 512, 512)
     gain = gain_ref[...]
 
     def keep(r, _):
         rows = pl.multiple_of(r * 64, 64)
-        own_ref[pl.ds(rows, 64), :] = normed_ref[pl.ds(half + rows, 64), :]
+        own_ref[pl.ds(rows, 64), :] = x_ref[pl.ds(half + rows, 64), :]
         return 0
 
     def norm(r, _):
-        rows = pl.ds(pl.multiple_of(r * 32, 32), 32)
-        normed_ref[rows, :] = layer_norm(normed_ref[rows, :].astype(F32), gain).astype(BF)
+        rows = pl.multiple_of(r * 64, 64)
+        values = x_ref[pl.ds(first + rows, 64), :].astype(F32)
+        normed_ref[pl.ds(rows, 64), :] = layer_norm(values, gain).astype(BF)
         return 0
 
     lax.fori_loop(0, 8, keep, 0)
-    lax.fori_loop(0, 32, norm, 0)
+    lax.fori_loop(0, 16, norm, 0)
 
 
 def widen_kernel(normed_ref, *refs):
@@ -127,8 +125,7 @@
 
     def write(half, ref, n, xx, yy):
         put_in_order(rows, w1, ref, half, n, xx, yy)
-        at = pl.multiple_of((yy * 4 + xx) * 32 + half * TX, 16)
-        texts[pl.ds(at, TX), :] = ref[n, rows[half] : rows[half] + TX, :]
+        texts[(yy * 4 + xx) * 2 + half] = ref[n, rows[half] : rows[half] + TX, :]
 
     each_piece(a_refs, b_refs, write)
 
@@ -181,10 +178,10 @@
         out_ref[rows, :] = (vector / jnp.maximum(length, 1.0)).astype(BF)
         return 0
 
-    lax.fori_loop(0, PAIRS // 128, embed, 0)
-
-
-def last_kernel(scale_ref, shift_ref, x_ref, own_ref, recv_ref, gain_ref, text_ref, out_ref):
+    lax.fori_loop(0, PAIRS // 256, embed, 0)
+
+
+def last_kernel(scale_ref, shift_ref, x_ref, own_ref, recv_ref, gain_ref, text_ref, other_ref, out_ref):
     gain = gain_ref[...]
     pooled = []
     for k in range(2):
@@ -200,16 +197,21 @@
     vector = jnp.concatenate(pooled + [jnp.zeros((6, D), F32)], axis=0)
     length = jnp.sqrt(jnp.sum(vector * vector, axis=-1, keepdims=True))
     emb = (vector / jnp.maximum(length, 1.0)).astype(BF)
-    scores = (
-        lax.dot_general(text_ref[...], emb, (((1,), (1,)), ((), ())), preferred_element_type=F32)
-        * scale_ref[0]
-        + shift_ref[0]
+    scores = jnp.concatenate(
+        [
+            lax.dot_general(ref[...], emb, (((1,), (1,)), ((), ())), preferred_element_type=F32)
+            for ref in (text_ref, other_ref)
+        ],
+        axis=0,
     )
+    scores = scores * scale_ref[0] + shift_ref[0]
     dp = lax.axis_index("y") * 16 + lax.axis_index("xh") * 8 + lax.axis_index("z")
-    slot = lax.axis_index("xl") * 4 + lax.axis_index("c") * 2
+    core = lax.axis_index("c")
+    slot = lax.axis_index("xl") * 4 + core * 2
     q = lax.broadcasted_iota(jnp.int32, (PAIRS, 8), 0)
     col = lax.broadcasted_iota(jnp.int32, (PAIRS, 8), 1)
-    q_dp, q_slot = (q // 64) * 8 + (q // 4) % 8, ((q // 32) % 2) * 4 + q % 4
+    q_dp = ((q % 256) // 32) * 8 + (q % 16) // 2
+    q_slot = ((q // 16) % 2) * 4 + jnp.where(q < 256, core, 1 - core) * 2 + q % 2
     own_pair = (q_dp == dp) & (q_slot == slot + col)
     value = jnp.where(own_pair, -scores, scores)
     terms = jnp.maximum(value, 0.0) + jnp.log1p(jnp.exp(-jnp.abs(value)))
@@ -219,7 +221,7 @@
     spread = jnp.where(q_slot == col, cols, 0.0)
     r = lax.broadcasted_iota(jnp.int32, (64, PAIRS), 0)
     c = lax.broadcasted_iota(jnp.int32, (64, PAIRS), 1)
-    owner = jnp.where((c // 64) * 8 + (c // 4) % 8 == r, 1.0, 0.0)
+    owner = jnp.where(((c % 256) // 32) * 8 + (c % 16) // 2 == r, 1.0, 0.0)
     col_part = jnp.dot(owner, spread, precision=lax.Precision.HIGHEST, preferred_element_type=F32)
     mr = lax.broadcasted_iota(jnp.int32, (64, 8), 0)
     mc = lax.broadcasted_iota(jnp.int32, (64, 8), 1)
@@ -230,7 +232,6 @@
         out_ref[:, m, :] = message
 
 
-ANY = pl.BlockSpec(memory_space=pl.ANY)
 VM = pl.BlockSpec(memory_space=pltpu.VMEM)
 SM = pl.BlockSpec(memory_space=pltpu.SMEM)
 
@@ -245,15 +246,15 @@
     sharpness_factor,
     score_offset_term,
 ):
-    xl = lax.axis_index("xl")
-    texts = lax.dynamic_slice_in_dim(caption_closing_activations, xl * 4, 4, 0)
+    first = lax.axis_index("xl") * 4 + lax.axis_index("c") * 2
+    texts = lax.dynamic_slice_in_dim(caption_closing_activations, first, 2, 0)
     weights = jnp.concatenate([widening_matrix, contracting_matrix.T], axis=0)
     weights = jnp.pad(weights, ((0, 0), (0, HID - weights.shape[1])))
     shard = jnp.concatenate([weights, texts], axis=0)
     along_z = gathered_along_z(shard)
     w1 = along_z[:, :18].reshape(144, HID)
     w2 = along_z[:, 18:36].reshape(144, HID)
-    tx = along_z[:, 36:].reshape(32, D)
+    tx = along_z[:, 36:].reshape(16, D)
     a = jnp.concatenate([w1[:W1A], tx[:TX], w2[:W2A]], axis=0)
     b = jnp.concatenate([w1[W1A:], tx[TX:], w2[W2A:]], axis=0)
 
@@ -265,18 +266,17 @@
     normed, own_rows = pl.pallas_call(
         norm_kernel,
         out_shape=(jax.ShapeDtypeStruct((1024, D), BF), jax.ShapeDtypeStruct((512, D), BF)),
-        in_specs=[ANY, VM],
+        in_specs=[VM, VM],
         out_specs=(VM, VM),
-        scratch_shapes=[pltpu.SemaphoreType.DMA],
         name="norm",
         cost_estimate=pl.CostEstimate(flops=20 * 1024 * D, transcendentals=0, bytes_accessed=6 << 20),
-        compiler_params=pltpu.CompilerParams(vmem_limit_bytes=8 << 20),
+        compiler_params=pltpu.CompilerParams(vmem_limit_bytes=12 << 20),
     )(picture_skip_activations, normaliser_multipliers[0:1])
 
     cost = pl.CostEstimate(flops=4 * 1024 * D * HID, transcendentals=0, bytes_accessed=12 << 20)
     units, texts = pl.pallas_call(
         widen_kernel,
-        out_shape=(jax.ShapeDtypeStruct((2, 1024, HID), BF), jax.ShapeDtypeStruct((PAIRS, D), BF)),
+        out_shape=(jax.ShapeDtypeStruct((2, 1024, HID), BF), jax.ShapeDtypeStruct((32, TX, D), BF)),
         in_specs=[VM] * 11,
         out_specs=(VM, VM),
         scratch_shapes=[pltpu.VMEM((2, D, HID), BF)],
@@ -286,13 +286,14 @@
     )(normed, *a1, *b1)
     text_emb = pl.pallas_call(
         text_kernel,
-        out_shape=jax.ShapeDtypeStruct((PAIRS, D), BF),
+        out_shape=jax.ShapeDtypeStruct((PAIRS // 2, D), BF),
         in_specs=[VM] * 3,
         out_specs=VM,
         name="text",
-        cost_estimate=pl.CostEstimate(flops=2 * PAIRS * D * D, transcendentals=0, bytes_accessed=5 << 20),
+        cost_estimate=pl.CostEstimate(flops=PAIRS * D * D, transcendentals=0, bytes_accessed=5 << 20),
         compiler_params=pltpu.CompilerParams(vmem_limit_bytes=12 << 20),
-    )(normaliser_multipliers[2:3], caption_mapping_matrix, texts)
+    )(normaliser_multipliers[2:3], caption_mapping_matrix, texts.reshape(PAIRS // 2, D))
+    other_emb = lax.ppermute(text_emb, "c", [(0, 1), (1, 0)])
     units, text_emb = lax.optimization_barrier((units, text_emb))
     half_cost = pl.CostEstimate(flops=2 * 1024 * D * HID, transcendentals=0, bytes_accessed=12 << 20)
     sent, second = pl.pallas_call(
@@ -317,11 +318,11 @@
     message = pl.pallas_call(
         last_kernel,
         out_shape=jax.ShapeDtypeStruct((64, 4, 16), F32),
-        in_specs=[SM, SM, VM, VM, VM, VM, VM],
+        in_specs=[SM, SM] + [VM] * 6,
         out_specs=VM,
         name="losses",
         compiler_params=pltpu.CompilerParams(vmem_limit_bytes=12 << 20),
-    )(sharpness_factor, score_offset_term, own_rows, own, received, normaliser_multipliers[1:2], text_emb)
+    )(sharpness_factor, score_offset_term, own_rows, own, received, normaliser_multipliers[1:2], text_emb, other_emb)
     arrived = jnp.sum(lax.all_to_all(message.reshape(256, 16), ALL, 0, 0, tiled=True), axis=0)
     return arrived[8:], arrived[:8]
 

time: 147 us -> 143 us (0.973)
  Pallas kernels: 29.7 us -> 24.8 us
  waiting for transfers between devices: 34 us -> 31.4 us
  local copies, waits for them, and re-layouts: 2.39 us -> 4.69 us
    pallas_call x1, Pallas kernels: 6.67 us -> 3.66 us  [on_device(): pl.pallas_call(norm_kernel, out_shape=(jax.ShapeDtypeStruct((1024, D), BF...]
    ppermute x31, waiting for transfers between devices: 34 us -> 31.4 us  [shifted(): lax.ppermute(array, axes, [(i, (i + by) % size) for i in range(size)])]
    unnamed x10 -> x8, local copies, waits for them, and re-layouts: 0.73 us -> 3.05 us
    pallas_call x1, Pallas kernels: 3.65 us -> 1.82 us  [on_device(): pl.pallas_call(text_kernel, out_shape=jax.ShapeDtypeStruct((PAIRS // 2, D...]
  transfers between devices with their start and end apart: 32 -> 33, of which waited for: 10 -> 10; matrix products, arithmetic and copies ran while one was open for 1% -> 1% of each run, Pallas kernels for 15% -> 12%
where the time goes in v1:
time: 143 us; the launch traced here: 141 us
  starting transfers between devices  52.8 us (37%)
  waiting for transfers between devices  31.4 us (22%)
  Pallas kernels  24.8 us (17%)
  blocking collectives  23.5 us (16%)
  local copies, waits for them, and re-layouts  4.69 us (3%)
  between operations  2.42 us (2%)
  other arithmetic  1.72 us (1%)
    ppermute x31, starting transfers between devices, shifted(): lax.ppermute(array, axes, [(i, (i + by) % size) for i in range(size)])  52.3 us
    ppermute x31, waiting for transfers between devices, shifted(): lax.ppermute(array, axes, [(i, (i + by) % size) for i in range(size)])  31.4 us
    all_to_all x1, blocking collectives, on_device(): lax.all_to_all(message.reshape(256, 16), ALL, 0, 0, tiled=True)  23.5 us
    pallas_call x1, Pallas kernels, on_device(): pl.pallas_call(widen_kernel, out_shape=(jax.ShapeDtypeStruct((2, 1024, HI...  8.18 us
    pallas_call x1, Pallas kernels, on_device(): pl.pallas_call(contract_sent_kernel, out_shape=(jax.ShapeDtypeStruct((512...  4.3 us
    pallas_call x1, Pallas kernels, on_device(): pl.pallas_call(contract_own_kernel, out_shape=jax.ShapeDtypeStruct((512,...  3.8 us
    pallas_call x1, Pallas kernels, on_device(): pl.pallas_call(norm_kernel, out_shape=(jax.ShapeDtypeStruct((1024, D), BF...  3.66 us
    unnamed x8, local copies, waits for them, and re-layouts  3.05 us
  transfers between devices with their start and end apart: 33, of which 10 were waited for; matrix products, arithmetic and copies ran while one was open for 1% of the time, Pallas kernels for 12%

profile of v1, /device:TPU:2, one launch (start us, length us, event | category | flops | bytes accessed | tf_op | source)
XLA Modules:
  0.0 141.4 jit_solution(2081713288447770736)
XLA Ops:
  0.7 0.7 copy-done
  1.4 0.9 fusion.2
  2.3 3.3 %collective-permute-start.2 = (bf16[38,1152]{1,0:T(8,128)(2,1)S(1)}, bf16[38,1152]{1,0:T(8,128)(2,1)S(1)}, u32[]{:S(2)}, u32[]{:S(2)}) collective-permute-start(bf16[38,1152]{1,0:T(8,128)(2,1)S(1)} %get-tuple-element.19), channel_id=1, source_target_pairs={{0,8},{4,12},{8,16},{12,20},{16,24},{20,28},{24,0},{28,4},{1,9},{5... | collective-permute-start | bytes 262664 | tf_op jit(solution)/shard_map/ppermute | solution.py:23
  5.7 3.1 %collective-permute-start.3 = (bf16[38,1152]{1,0:T(8,128)(2,1)S(1)}, bf16[38,1152]{1,0:T(8,128)(2,1)S(1)}, u32[]{:S(2)}, u32[]{:S(2)}) collective-permute-start(bf16[38,1152]{1,0:T(8,128)(2,1)S(1)} %get-tuple-element.19), channel_id=1, source_target_pairs={{0,24},{4,28},{8,0},{12,4},{16,8},{20,12},{24,16},{28,20},{1,25},{... | collective-permute-start | bytes 262664 | tf_op jit(solution)/shard_map/ppermute | solution.py:23
  8.8 1.0 collective-permute-start
  9.8 2.2 %collective-permute-start.1 = (bf16[38,1152]{1,0:T(8,128)(2,1)S(1)}, bf16[38,1152]{1,0:T(8,128)(2,1)S(1)}, u32[]{:S(2)}, u32[]{:S(2)}) collective-permute-start(bf16[38,1152]{1,0:T(8,128)(2,1)S(1)} %get-tuple-element.19), channel_id=1, source_target_pairs={{0,28},{4,0},{8,4},{12,8},{16,12},{20,16},{24,20},{28,24},{1,29},{... | collective-permute-start | bytes 262664 | tf_op jit(solution)/shard_map/ppermute | solution.py:23
  12.0 2.9 %collective-permute-start.4 = (bf16[38,1152]{1,0:T(8,128)(2,1)S(1)}, bf16[38,1152]{1,0:T(8,128)(2,1)S(1)}, u32[]{:S(2)}, u32[]{:S(2)}) collective-permute-start(bf16[38,1152]{1,0:T(8,128)(2,1)S(1)} %collective-permute-done.2), channel_id=1, source_target_pairs={{0,4},{4,8},{8,12},{12,16},{16,20},{20,24},{24,28},{28,0},{1,5},{5... | collective-permute-start | bytes 262664 | tf_op jit(solution)/shard_map/ppermute | solution.py:23
  14.9 0.2 collective-permute-done.3
  15.1 2.5 %collective-permute-start.5 = (bf16[38,1152]{1,0:T(8,128)(2,1)S(1)}, bf16[38,1152]{1,0:T(8,128)(2,1)S(1)}, u32[]{:S(2)}, u32[]{:S(2)}) collective-permute-start(bf16[38,1152]{1,0:T(8,128)(2,1)S(1)} %collective-permute-done.3), channel_id=1, source_target_pairs={{0,28},{4,0},{8,4},{12,8},{16,12},{20,16},{24,20},{28,24},{1,29},{... | collective-permute-start | bytes 262664 | tf_op jit(solution)/shard_map/ppermute | solution.py:23
  17.7 1.7 %collective-permute-done.4 = bf16[38,1152]{1,0:T(8,128)(2,1)S(1)} collective-permute-done((bf16[38,1152]{1,0:T(8,128)(2,1)S(1)}, bf16[38,1152]{1,0:T(8,128)(2,1)S(1)}, u32[]{:S(2)}, u32[]{:S(2)}) %collective-permute-start.4) | collective-permute-done | bytes 87584 | tf_op jit(solution)/shard_map/ppermute | solution.py:23
  19.4 2.3 %collective-permute-done.5 = bf16[38,1152]{1,0:T(8,128)(2,1)S(1)} collective-permute-done((bf16[38,1152]{1,0:T(8,128)(2,1)S(1)}, bf16[38,1152]{1,0:T(8,128)(2,1)S(1)}, u32[]{:S(2)}, u32[]{:S(2)}) %collective-permute-start.5) | collective-permute-done | bytes 87584 | tf_op jit(solution)/shard_map/ppermute | solution.py:23
  21.7 0.6 collective-permute-done.6
  22.9 0.6 collective-permute-start.9
  23.5 1.5 %collective-permute-start.7 = (bf16[152,1152]{1,0:T(8,128)(2,1)S(1)}, bf16[152,1152]{1,0:T(8,128)(2,1)S(1)}, u32[]{:S(2)}, u32[]{:S(2)}) collective-permute-start(bf16[152,1152]{1,0:T(8,128)(2,1)S(1)} %pad_maximum_fusion.4), channel_id=1, source_target_pairs={{0,2},{2,32},{32,34},{34,0},{1,3},{3,33},{33,35},{35,1},{4,6},{6,3... | collective-permute-start | bytes 1050632 | tf_op jit(solution)/shard_map/ppermute | solution.py:23
  25.1 3.1 %collective-permute-start.16 = (bf16[152,1152]{1,0:T(8,128)(2,1)S(1)}, bf16[152,1152]{1,0:T(8,128)(2,1)S(1)}, u32[]{:S(2)}, u32[]{:S(2)}) collective-permute-start(bf16[152,1152]{1,0:T(8,128)(2,1)S(1)} %pad_maximum_fusion.5), channel_id=1, source_target_pairs={{0,192},{64,0},{128,64},{192,128},{1,193},{65,1},{129,65},{193,129... | collective-permute-start | bytes 1050632 | tf_op jit(solution)/shard_map/ppermute | solution.py:23
  28.2 4.5 %collective-permute-done.7 = bf16[152,1152]{1,0:T(8,128)(2,1)S(1)} collective-permute-done((bf16[152,1152]{1,0:T(8,128)(2,1)S(1)}, bf16[152,1152]{1,0:T(8,128)(2,1)S(1)}, u32[]{:S(2)}, u32[]{:S(2)}) %collective-permute-start.7) | collective-permute-done | bytes 350240 | tf_op jit(solution)/shard_map/ppermute | solution.py:23
  32.7 0.6 collective-permute-start.8
  33.3 3.7 %collective-permute-done.14 = bf16[152,1152]{1,0:T(8,128)(2,1)S(1)} collective-permute-done((bf16[152,1152]{1,0:T(8,128)(2,1)S(1)}, bf16[152,1152]{1,0:T(8,128)(2,1)S(1)}, u32[]{:S(2)}, u32[]{:S(2)}) %collective-permute-start.14) | collective-permute-done | bytes 350240 | tf_op jit(solution)/shard_map/ppermute | solution.py:23
  37.1 1.6 %collective-permute-start.21 = (bf16[64,1152]{1,0:T(8,128)(2,1)S(1)}, bf16[64,1152]{1,0:T(8,128)(2,1)S(1)}, u32[]{:S(2)}, u32[]{:S(2)}) collective-permute-start(bf16[64,1152]{1,0:T(8,128)(2,1)S(1)} %get-tuple-element.26), channel_id=1, source_target_pairs={{0,34},{2,0},{32,2},{34,32},{1,35},{3,1},{33,3},{35,33},{4,38},{6,... | collective-permute-start | bytes 442376 | tf_op jit(solution)/shard_map/ppermute | solution.py:23
  38.8 3.5 %collective-permute-start.26 = (bf16[80,1152]{1,0:T(8,128)(2,1)S(1)}, bf16[80,1152]{1,0:T(8,128)(2,1)S(1)}, u32[]{:S(2)}, u32[]{:S(2)}) collective-permute-start(bf16[80,1152]{1,0:T(8,128)(2,1)S(1)} %get-tuple-element.24), channel_id=1, source_target_pairs={{0,192},{64,0},{128,64},{192,128},{1,193},{65,1},{129,65},{193,129... | collective-permute-start | bytes 552968 | tf_op jit(solution)/shard_map/ppermute | solution.py:23
  42.4 1.3 collective-permute-done.15
  43.8 1.6 %collective-permute-start.17 = (bf16[4,72,1152]{2,1,0:T(8,128)(2,1)S(1)}, bf16[4,72,1152]{2,1,0:T(8,128)(2,1)S(1)}, u32[]{:S(2)}, u32[]{:S(2)}) collective-permute-start(bf16[4,72,1152]{2,1,0:T(8,128)(2,1)S(1)} %pad_maximum_fusion.2.refs_5_), channel_id=1, source_target_pairs={{0,2},{2,32},{32,34},{34,0},{1,3},{3,33},{33,35},{35,1},{4,6},{6,3... | collective-permute-start | bytes 1990664 | tf_op jit(solution)/shard_map/ppermute | solution.py:23
  45.3 0.5 collective-permute-start.18
  45.9 0.1 pad_maximum_fusion.refs_0_
  46.1 0.1 pad_maximum_fusion.1.refs_5_
  46.2 2.0 %collective-permute-start.27 = (bf16[4,80,1152]{2,1,0:T(8,128)(2,1)S(1)}, bf16[4,80,1152]{2,1,0:T(8,128)(2,1)S(1)}, u32[]{:S(2)}, u32[]{:S(2)}) collective-permute-start(bf16[4,80,1152]{2,1,0:T(8,128)(2,1)S(1)} %pad_maximum_fusion.1.refs_5_), channel_id=1, source_target_pairs={{0,2},{2,32},{32,34},{34,0},{1,3},{3,33},{33,35},{35,1},{4,6},{6,3... | collective-permute-start | bytes 2211848 | tf_op jit(solution)/shard_map/ppermute | solution.py:23
  48.2 3.2 %collective-permute-start.11 = (bf16[4,88,1152]{2,1,0:T(8,128)(2,1)S(1)}, bf16[4,88,1152]{2,1,0:T(8,128)(2,1)S(1)}, u32[]{:S(2)}, u32[]{:S(2)}) collective-permute-start(bf16[4,88,1152]{2,1,0:T(8,128)(2,1)S(1)} %pad_maximum_fusion.refs_0_), channel_id=1, source_target_pairs={{0,192},{64,0},{128,64},{192,128},{1,193},{65,1},{129,65},{193,129... | collective-permute-start | bytes 2433032 | tf_op jit(solution)/shard_map/ppermute | solution.py:23
  51.5 10.1 %collective-permute-done.17.refs_6_ = bf16[4,72,1152]{2,1,0:T(8,128)(2,1)S(1)} collective-permute-done((bf16[4,72,1152]{2,1,0:T(8,128)(2,1)S(1)}, bf16[4,72,1152]{2,1,0:T(8,128)(2,1)S(1)}, u32[]{:S(2)}, u32[]{:S(2)}) %collective-permute-start.17) | collective-permute-done | bytes 663584 | tf_op jit(solution)/shard_map/ppermute | solution.py:23
  61.6 3.2 %collective-permute-start.23 = (bf16[4,64,1152]{2,1,0:T(8,128)(2,1)S(1)}, bf16[4,64,1152]{2,1,0:T(8,128)(2,1)S(1)}, u32[]{:S(2)}, u32[]{:S(2)}) collective-permute-start(bf16[4,64,1152]{2,1,0:T(8,128)(2,1)S(1)} %pad_maximum_fusion.3.refs_0_), channel_id=1, source_target_pairs={{0,192},{64,0},{128,64},{192,128},{1,193},{65,1},{129,65},{193,129... | collective-permute-start | bytes 1769480 | tf_op jit(solution)/shard_map/ppermute | solution.py:23
  64.9 3.4 %collective-permute-done.10.refs_1_ = bf16[4,88,1152]{2,1,0:T(8,128)(2,1)S(1)} collective-permute-done((bf16[4,88,1152]{2,1,0:T(8,128)(2,1)S(1)}, bf16[4,88,1152]{2,1,0:T(8,128)(2,1)S(1)}, u32[]{:S(2)}, u32[]{:S(2)}) %collective-permute-start.10) | collective-permute-done | bytes 811040 | tf_op jit(solution)/shard_map/ppermute | solution.py:23
  68.2 2.9 %collective-permute-start.28 = (bf16[4,80,1152]{2,1,0:T(8,128)(2,1)S(1)}, bf16[4,80,1152]{2,1,0:T(8,128)(2,1)S(1)}, u32[]{:S(2)}, u32[]{:S(2)}) collective-permute-start(bf16[4,80,1152]{2,1,0:T(8,128)(2,1)S(1)} %pad_maximum_fusion.1.refs_5_), channel_id=1, source_target_pairs={{0,34},{2,0},{32,2},{34,32},{1,35},{3,1},{33,3},{35,33},{4,38},{6,... | collective-permute-start | bytes 2211848 | tf_op jit(solution)/shard_map/ppermute | solution.py:23
  71.2 0.4 collective-permute-start.19
  71.7 3.7 %collective-permute-done.22.refs_1_ = bf16[4,64,1152]{2,1,0:T(8,128)(2,1)S(1)} collective-permute-done((bf16[4,64,1152]{2,1,0:T(8,128)(2,1)S(1)}, bf16[4,64,1152]{2,1,0:T(8,128)(2,1)S(1)}, u32[]{:S(2)}, u32[]{:S(2)}) %collective-permute-start.22) | collective-permute-done | bytes 589856 | tf_op jit(solution)/shard_map/ppermute | solution.py:23
  75.3 3.7 %collective-permute-start.20 = (bf16[2,72,1152]{2,1,0:T(8,128)(2,1)S(1)}, bf16[2,72,1152]{2,1,0:T(8,128)(2,1)S(1)}, u32[]{:S(2)}, u32[]{:S(2)}) collective-permute-start(bf16[2,72,1152]{2,1,0:T(8,128)(2,1)S(1)} %slice.150), channel_id=1, source_target_pairs={{0,34},{2,0},{32,2},{34,32},{1,35},{3,1},{33,3},{35,33},{4,38},{6,... | collective-permute-start | bytes 995336 | tf_op jit(solution)/shard_map/ppermute | solution.py:23
  79.0 3.2 %collective-permute-start.13 = (bf16[2,88,1152]{2,1,0:T(8,128)(2,1)S(1)}, bf16[2,88,1152]{2,1,0:T(8,128)(2,1)S(1)}, u32[]{:S(2)}, u32[]{:S(2)}) collective-permute-start(bf16[2,88,1152]{2,1,0:T(8,128)(2,1)S(1)} %slice.143), channel_id=1, source_target_pairs={{0,192},{64,0},{128,64},{192,128},{1,193},{65,1},{129,65},{193,129... | collective-permute-start | bytes 1216520 | tf_op jit(solution)/shard_map/ppermute | solution.py:23
  82.3 2.3 %copy-done.1 = bf16[2048,1152]{1,0:T(8,128)(2,1)S(1)} copy-done((bf16[2048,1152]{1,0:T(8,128)(2,1)S(1)}, bf16[2048,1152]{1,0:T(8,128)(2,1)}, u32[]{:S(2)}) %copy-start.1) | copy-done | bytes 4718616
  84.6 3.7 %norm.1 = (bf16[1024,1152]{1,0:T(8,128)(2,1)S(1)}, bf16[512,1152]{1,0:T(8,128)(2,1)S(1)}) custom-call(bf16[2048,1152]{1,0:T(8,128)(2,1)S(1)} %copy-done.1, f32[1,1152]{1,0:T(1,128)S(1)} %get-tuple-element.37.gain_ref), custom_call_target="tpu_custom_call" | custom-call | flops 23592960 | bytes 6291456 | tf_op jit(solution)/shard_map/norm/pallas_call | solution.py:266
  88.6 3.3 %collective-permute-start.25 = (bf16[2,64,1152]{2,1,0:T(8,128)(2,1)S(1)}, bf16[2,64,1152]{2,1,0:T(8,128)(2,1)S(1)}, u32[]{:S(2)}, u32[]{:S(2)}) collective-permute-start(bf16[2,64,1152]{2,1,0:T(8,128)(2,1)S(1)} %slice.154), channel_id=1, source_target_pairs={{0,192},{64,0},{128,64},{192,128},{1,193},{65,1},{129,65},{193,129... | collective-permute-start | bytes 884744 | tf_op jit(solution)/shard_map/ppermute | solution.py:23
  91.9 2.0 %collective-permute-start.29 = (bf16[2,80,1152]{2,1,0:T(8,128)(2,1)S(1)}, bf16[2,80,1152]{2,1,0:T(8,128)(2,1)S(1)}, u32[]{:S(2)}, u32[]{:S(2)}) collective-permute-start(bf16[2,80,1152]{2,1,0:T(8,128)(2,1)S(1)} %slice.157), channel_id=1, source_target_pairs={{0,2},{2,32},{32,34},{34,0},{1,3},{3,33},{33,35},{35,1},{4,6},{6,3... | collective-permute-start | bytes 1105928 | tf_op jit(solution)/shard_map/ppermute | solution.py:23
  93.9 8.2 %widen.1 = (bf16[2,1024,1152]{2,1,0:T(8,128)(2,1)S(1)}, bf16[32,8,1152]{2,1,0:T(8,128)(2,1)S(1)}) custom-call(bf16[1024,1152]{1,0:T(8,128)(2,1)S(1)} %get-tuple-element.11.normed_ref, bf16[4,88,1152]{2,1,0:T(8,128)(2,1)S(1)} %pad_maximum_fusion.refs_0_, bf16[4,88,1152]{2,1,0:T(8,128)(2,1)S(1)} %collective-permute-done.10.refs_1_, ...), custom_call_target="tpu_custom_call" | custom-call | flops 5435817984 | bytes 12582912 | tf_op jit(solution)/shard_map/widen/pallas_call | solution.py:277
  102.1 1.8 %text.1.text_ref = bf16[256,1152]{1,0:T(8,128)(2,1)S(1)} custom-call(f32[1,1152]{1,0:T(1,128)S(1)} %get-tuple-element.38.gain_ref, bf16[1152,1152]{1,0:T(8,128)(2,1)S(1)} %copy-done.2, bf16[256,1152]{1,0:T(8,128)(2,1)S(1)} %bitcast.49), custom_call_target="tpu_custom_call" | custom-call | flops 679477248 | bytes 5242880 | tf_op jit(solution)/shard_map/text/pallas_call | solution.py:287
  104.0 4.3 %contract_sent.1 = (bf16[512,1152]{1,0:T(8,128)(2,1)S(1)}, bf16[2,1152,1152]{2,1,0:T(8,128)(2,1)S(1)}) custom-call(bf16[2,1024,1152]{2,1,0:T(8,128)(2,1)S(1)} %get-tuple-element.14.h, bf16[4,64,1152]{2,1,0:T(8,128)(2,1)S(1)} %pad_maximum_fusion.3.refs_0_, bf16[4,64,1152]{2,1,0:T(8,128)(2,1)S(1)} %collective-permute-done.22.refs_1_, ...), custom_call_target="tpu_custom_call" | custom-call | flops 2717908992 | bytes 12582912 | tf_op jit(solution)/shard_map/contract_sent/pallas_call | solution.py:299
  108.4 0.5 collective-permute-start.32
  110.2 3.8 %contract_own.1.own_ref = f32[512,1152]{1,0:T(8,128)S(1)} custom-call(bf16[2,1024,1152]{2,1,0:T(8,128)(2,1)S(1)} %get-tuple-element.14.h, bf16[2,1152,1152]{2,1,0:T(8,128)(2,1)S(1)} %get-tuple-element.15.w2), custom_call_target="tpu_custom_call" | custom-call | flops 2717908992 | bytes 12582912 | tf_op jit(solution)/shard_map/contract_own/pallas_call | solution.py:309
  114.0 3.0 %losses.1 = f32[64,4,16]{2,1,0:T(4,128)S(1)} custom-call(f32[1]{0:T(128)S(6)} %copy.19.scale_ref, f32[1]{0:T(128)S(6)} %copy.20.shift_ref, bf16[512,1152]{1,0:T(8,128)(2,1)S(1)} %get-tuple-element.10.x_ref, f32[512,1152]{1,0:T(8,128)S(1)} %contract_own.1.own_ref, bf16[512,1152]{1,0:T(8,128)(2,1)S(1)} %collective-permute-done.31.recv_ref, ...), custom_call_target="tpu_custom_call" | custom-call | tf_op jit(solution)/shard_map/losses/pallas_call | solution.py:318
  117.0 23.5 %all_to_all.9 = f32[256,1,16]{2,1,0:T(1,128)S(1)} all-to-all(f32[256,1,16]{2,1,0:T(1,128)S(1)} %bitcast.50), channel_id=1, replica_groups=mesh['y'=4,'xh'=2,'z'=8,'xl'=2,'c'=2] {'y','xh','z','xl','c'}, dimensions={0} | all-to-all | bytes 32768 | tf_op jit(solution)/shard_map/all_to_all | solution.py:326
  140.5 0.3 reduce_sum.9
  140.8 0.6 fusion.8
  (81 shorter events, 1.8 us)
Async XLA Ops:
  0.6 0.7 copy-start
  2.3 9.7 %collective-permute-start.2 = (bf16[38,1152]{1,0:T(8,128)(2,1)S(1)}, bf16[38,1152]{1,0:T(8,128)(2,1)S(1)}, u32[]{:S(2)}, u32[]{:S(2)}) collective-permute-start(bf16[38,1152]{1,0:T(8,128)(2,1)S(1)} %get-tuple-element.19), channel_id=1, source_target_pairs={{0,8},{4,12},{8,16},{12,20},{16,24},{20,28},{24,0},{28,4},{1,9},{5... | collective-permute-start | bytes 262664 | tf_op jit(solution)/shard_map/ppermute | solution.py:23
  5.7 9.4 %collective-permute-start.3 = (bf16[38,1152]{1,0:T(8,128)(2,1)S(1)}, bf16[38,1152]{1,0:T(8,128)(2,1)S(1)}, u32[]{:S(2)}, u32[]{:S(2)}) collective-permute-start(bf16[38,1152]{1,0:T(8,128)(2,1)S(1)} %get-tuple-element.19), channel_id=1, source_target_pairs={{0,24},{4,28},{8,0},{12,4},{16,8},{20,12},{24,16},{28,20},{1,25},{... | collective-permute-start | bytes 262664 | tf_op jit(solution)/shard_map/ppermute | solution.py:23
  8.8 8.8 %collective-permute-start = (bf16[38,1152]{1,0:T(8,128)(2,1)S(1)}, bf16[38,1152]{1,0:T(8,128)(2,1)S(1)}, u32[]{:S(2)}, u32[]{:S(2)}) collective-permute-start(bf16[38,1152]{1,0:T(8,128)(2,1)S(1)} %get-tuple-element.19), channel_id=1, source_target_pairs={{0,4},{4,8},{8,12},{12,16},{16,20},{20,24},{24,28},{28,0},{1,5},{5... | collective-permute-start | bytes 262664 | tf_op jit(solution)/shard_map/ppermute | solution.py:23
  9.8 7.8 %collective-permute-start.1 = (bf16[38,1152]{1,0:T(8,128)(2,1)S(1)}, bf16[38,1152]{1,0:T(8,128)(2,1)S(1)}, u32[]{:S(2)}, u32[]{:S(2)}) collective-permute-start(bf16[38,1152]{1,0:T(8,128)(2,1)S(1)} %get-tuple-element.19), channel_id=1, source_target_pairs={{0,28},{4,0},{8,4},{12,8},{16,12},{20,16},{24,20},{28,24},{1,29},{... | collective-permute-start | bytes 262664 | tf_op jit(solution)/shard_map/ppermute | solution.py:23
  12.0 7.3 %collective-permute-start.4 = (bf16[38,1152]{1,0:T(8,128)(2,1)S(1)}, bf16[38,1152]{1,0:T(8,128)(2,1)S(1)}, u32[]{:S(2)}, u32[]{:S(2)}) collective-permute-start(bf16[38,1152]{1,0:T(8,128)(2,1)S(1)} %collective-permute-done.2), channel_id=1, source_target_pairs={{0,4},{4,8},{8,12},{12,16},{16,20},{20,24},{24,28},{28,0},{1,5},{5... | collective-permute-start | bytes 262664 | tf_op jit(solution)/shard_map/ppermute | solution.py:23
  14.9 7.4 %collective-permute-start.6 = (bf16[38,1152]{1,0:T(8,128)(2,1)S(1)}, bf16[38,1152]{1,0:T(8,128)(2,1)S(1)}, u32[]{:S(2)}, u32[]{:S(2)}) collective-permute-start(bf16[38,1152]{1,0:T(8,128)(2,1)S(1)} %collective-permute-done.2), channel_id=1, source_target_pairs={{0,8},{4,12},{8,16},{12,20},{16,24},{20,28},{24,0},{28,4},{1,9},{5... | collective-permute-start | bytes 262664 | tf_op jit(solution)/shard_map/ppermute | solution.py:23
  15.1 6.6 %collective-permute-start.5 = (bf16[38,1152]{1,0:T(8,128)(2,1)S(1)}, bf16[38,1152]{1,0:T(8,128)(2,1)S(1)}, u32[]{:S(2)}, u32[]{:S(2)}) collective-permute-start(bf16[38,1152]{1,0:T(8,128)(2,1)S(1)} %collective-permute-done.3), channel_id=1, source_target_pairs={{0,28},{4,0},{8,4},{12,8},{16,12},{20,16},{24,20},{28,24},{1,29},{... | collective-permute-start | bytes 262664 | tf_op jit(solution)/shard_map/ppermute | solution.py:23
  22.9 14.3 %collective-permute-start.9 = (bf16[152,1152]{1,0:T(8,128)(2,1)S(1)}, bf16[152,1152]{1,0:T(8,128)(2,1)S(1)}, u32[]{:S(2)}, u32[]{:S(2)}) collective-permute-start(bf16[152,1152]{1,0:T(8,128)(2,1)S(1)} %pad_maximum_fusion.4), channel_id=1, source_target_pairs={{0,34},{2,0},{32,2},{34,32},{1,35},{3,1},{33,3},{35,33},{4,38},{6,... | collective-permute-start | bytes 1050632 | tf_op jit(solution)/shard_map/ppermute | solution.py:23
  23.5 9.2 %collective-permute-start.7 = (bf16[152,1152]{1,0:T(8,128)(2,1)S(1)}, bf16[152,1152]{1,0:T(8,128)(2,1)S(1)}, u32[]{:S(2)}, u32[]{:S(2)}) collective-permute-start(bf16[152,1152]{1,0:T(8,128)(2,1)S(1)} %pad_maximum_fusion.4), channel_id=1, source_target_pairs={{0,2},{2,32},{32,34},{34,0},{1,3},{3,33},{33,35},{35,1},{4,6},{6,3... | collective-permute-start | bytes 1050632 | tf_op jit(solution)/shard_map/ppermute | solution.py:23
  25.1 13.7 %collective-permute-start.16 = (bf16[152,1152]{1,0:T(8,128)(2,1)S(1)}, bf16[152,1152]{1,0:T(8,128)(2,1)S(1)}, u32[]{:S(2)}, u32[]{:S(2)}) collective-permute-start(bf16[152,1152]{1,0:T(8,128)(2,1)S(1)} %pad_maximum_fusion.5), channel_id=1, source_target_pairs={{0,192},{64,0},{128,64},{192,128},{1,193},{65,1},{129,65},{193,129... | collective-permute-start | bytes 1050632 | tf_op jit(solution)/shard_map/ppermute | solution.py:23
  28.2 8.8 %collective-permute-start.14 = (bf16[152,1152]{1,0:T(8,128)(2,1)S(1)}, bf16[152,1152]{1,0:T(8,128)(2,1)S(1)}, u32[]{:S(2)}, u32[]{:S(2)}) collective-permute-start(bf16[152,1152]{1,0:T(8,128)(2,1)S(1)} %pad_maximum_fusion.5), channel_id=1, source_target_pairs={{0,64},{64,128},{128,192},{192,0},{1,65},{65,129},{129,193},{193,1... | collective-permute-start | bytes 1050632 | tf_op jit(solution)/shard_map/ppermute | solution.py:23
  32.7 13.2 %collective-permute-start.8 = (bf16[88,1152]{1,0:T(8,128)(2,1)S(1)}, bf16[88,1152]{1,0:T(8,128)(2,1)S(1)}, u32[]{:S(2)}, u32[]{:S(2)}) collective-permute-start(bf16[88,1152]{1,0:T(8,128)(2,1)S(1)} %get-tuple-element.31), channel_id=1, source_target_pairs={{0,2},{2,32},{32,34},{34,0},{1,3},{3,33},{33,35},{35,1},{4,6},{6,3... | collective-permute-start | bytes 608264 | tf_op jit(solution)/shard_map/ppermute | solution.py:23
  37.0 6.6 %collective-permute-start.15 = (bf16[72,1152]{1,0:T(8,128)(2,1)S(1)}, bf16[72,1152]{1,0:T(8,128)(2,1)S(1)}, u32[]{:S(2)}, u32[]{:S(2)}) collective-permute-start(bf16[72,1152]{1,0:T(8,128)(2,1)S(1)} %get-tuple-element.29), channel_id=1, source_target_pairs={{0,64},{64,128},{128,192},{192,0},{1,65},{65,129},{129,193},{193,1... | collective-permute-start | bytes 497672 | tf_op jit(solution)/shard_map/ppermute | solution.py:23
  37.1 11.0 %collective-permute-start.21 = (bf16[64,1152]{1,0:T(8,128)(2,1)S(1)}, bf16[64,1152]{1,0:T(8,128)(2,1)S(1)}, u32[]{:S(2)}, u32[]{:S(2)}) collective-permute-start(bf16[64,1152]{1,0:T(8,128)(2,1)S(1)} %get-tuple-element.26), channel_id=1, source_target_pairs={{0,34},{2,0},{32,2},{34,32},{1,35},{3,1},{33,3},{35,33},{4,38},{6,... | collective-permute-start | bytes 442376 | tf_op jit(solution)/shard_map/ppermute | solution.py:23
  38.8 7.3 %collective-permute-start.26 = (bf16[80,1152]{1,0:T(8,128)(2,1)S(1)}, bf16[80,1152]{1,0:T(8,128)(2,1)S(1)}, u32[]{:S(2)}, u32[]{:S(2)}) collective-permute-start(bf16[80,1152]{1,0:T(8,128)(2,1)S(1)} %get-tuple-element.24), channel_id=1, source_target_pairs={{0,192},{64,0},{128,64},{192,128},{1,193},{65,1},{129,65},{193,129... | collective-permute-start | bytes 552968 | tf_op jit(solution)/shard_map/ppermute | solution.py:23
  43.8 17.9 %collective-permute-start.17 = (bf16[4,72,1152]{2,1,0:T(8,128)(2,1)S(1)}, bf16[4,72,1152]{2,1,0:T(8,128)(2,1)S(1)}, u32[]{:S(2)}, u32[]{:S(2)}) collective-permute-start(bf16[4,72,1152]{2,1,0:T(8,128)(2,1)S(1)} %pad_maximum_fusion.2.refs_5_), channel_id=1, source_target_pairs={{0,2},{2,32},{32,34},{34,0},{1,3},{3,33},{33,35},{35,1},{4,6},{6,3... | collective-permute-start | bytes 1990664 | tf_op jit(solution)/shard_map/ppermute | solution.py:23
  45.3 16.3 %collective-permute-start.18 = (bf16[4,72,1152]{2,1,0:T(8,128)(2,1)S(1)}, bf16[4,72,1152]{2,1,0:T(8,128)(2,1)S(1)}, u32[]{:S(2)}, u32[]{:S(2)}) collective-permute-start(bf16[4,72,1152]{2,1,0:T(8,128)(2,1)S(1)} %pad_maximum_fusion.2.refs_5_), channel_id=1, source_target_pairs={{0,34},{2,0},{32,2},{34,32},{1,35},{3,1},{33,3},{35,33},{4,38},{6,... | collective-permute-start | bytes 1990664 | tf_op jit(solution)/shard_map/ppermute | solution.py:23
  46.0 22.2 %collective-permute-start.10 = (bf16[4,88,1152]{2,1,0:T(8,128)(2,1)S(1)}, bf16[4,88,1152]{2,1,0:T(8,128)(2,1)S(1)}, u32[]{:S(2)}, u32[]{:S(2)}) collective-permute-start(bf16[4,88,1152]{2,1,0:T(8,128)(2,1)S(1)} %pad_maximum_fusion.refs_0_), channel_id=1, source_target_pairs={{0,64},{64,128},{128,192},{192,0},{1,65},{65,129},{129,193},{193,1... | collective-permute-start | bytes 2433032 | tf_op jit(solution)/shard_map/ppermute | solution.py:23
  46.2 36.1 %copy-start.3 = (f32[3,1152]{1,0:T(4,128)S(1)}, f32[3,1152]{1,0:T(4,128)}, u32[]{:S(2)}) copy-start(f32[3,1152]{1,0:T(4,128)} %param.10) | copy-start | bytes 41476
  46.2 32.8 %collective-permute-start.27 = (bf16[4,80,1152]{2,1,0:T(8,128)(2,1)S(1)}, bf16[4,80,1152]{2,1,0:T(8,128)(2,1)S(1)}, u32[]{:S(2)}, u32[]{:S(2)}) collective-permute-start(bf16[4,80,1152]{2,1,0:T(8,128)(2,1)S(1)} %pad_maximum_fusion.1.refs_5_), channel_id=1, source_target_pairs={{0,2},{2,32},{32,34},{34,0},{1,3},{3,33},{33,35},{35,1},{4,6},{6,3... | collective-permute-start | bytes 2211848 | tf_op jit(solution)/shard_map/ppermute | solution.py:23
  48.2 23.0 %collective-permute-start.11 = (bf16[4,88,1152]{2,1,0:T(8,128)(2,1)S(1)}, bf16[4,88,1152]{2,1,0:T(8,128)(2,1)S(1)}, u32[]{:S(2)}, u32[]{:S(2)}) collective-permute-start(bf16[4,88,1152]{2,1,0:T(8,128)(2,1)S(1)} %pad_maximum_fusion.refs_0_), channel_id=1, source_target_pairs={{0,192},{64,0},{128,64},{192,128},{1,193},{65,1},{129,65},{193,129... | collective-permute-start | bytes 2433032 | tf_op jit(solution)/shard_map/ppermute | solution.py:23
  61.6 13.7 %collective-permute-start.22 = (bf16[4,64,1152]{2,1,0:T(8,128)(2,1)S(1)}, bf16[4,64,1152]{2,1,0:T(8,128)(2,1)S(1)}, u32[]{:S(2)}, u32[]{:S(2)}) collective-permute-start(bf16[4,64,1152]{2,1,0:T(8,128)(2,1)S(1)} %pad_maximum_fusion.3.refs_0_), channel_id=1, source_target_pairs={{0,64},{64,128},{128,192},{192,0},{1,65},{65,129},{129,193},{193,1... | collective-permute-start | bytes 1769480 | tf_op jit(solution)/shard_map/ppermute | solution.py:23
  61.6 17.4 %collective-permute-start.23 = (bf16[4,64,1152]{2,1,0:T(8,128)(2,1)S(1)}, bf16[4,64,1152]{2,1,0:T(8,128)(2,1)S(1)}, u32[]{:S(2)}, u32[]{:S(2)}) collective-permute-start(bf16[4,64,1152]{2,1,0:T(8,128)(2,1)S(1)} %pad_maximum_fusion.3.refs_0_), channel_id=1, source_target_pairs={{0,192},{64,0},{128,64},{192,128},{1,193},{65,1},{129,65},{193,129... | collective-permute-start | bytes 1769480 | tf_op jit(solution)/shard_map/ppermute | solution.py:23
  68.2 20.2 %collective-permute-start.28 = (bf16[4,80,1152]{2,1,0:T(8,128)(2,1)S(1)}, bf16[4,80,1152]{2,1,0:T(8,128)(2,1)S(1)}, u32[]{:S(2)}, u32[]{:S(2)}) collective-permute-start(bf16[4,80,1152]{2,1,0:T(8,128)(2,1)S(1)} %pad_maximum_fusion.1.refs_5_), channel_id=1, source_target_pairs={{0,34},{2,0},{32,2},{34,32},{1,35},{3,1},{33,3},{35,33},{4,38},{6,... | collective-permute-start | bytes 2211848 | tf_op jit(solution)/shard_map/ppermute | solution.py:23
  71.2 17.3 %collective-permute-start.19 = (bf16[2,72,1152]{2,1,0:T(8,128)(2,1)S(1)}, bf16[2,72,1152]{2,1,0:T(8,128)(2,1)S(1)}, u32[]{:S(2)}, u32[]{:S(2)}) collective-permute-start(bf16[2,72,1152]{2,1,0:T(8,128)(2,1)S(1)} %slice.149), channel_id=1, source_target_pairs={{0,2},{2,32},{32,34},{34,0},{1,3},{3,33},{33,35},{35,1},{4,6},{6,3... | collective-permute-start | bytes 995336 | tf_op jit(solution)/shard_map/ppermute | solution.py:23
  75.3 16.5 %collective-permute-start.20 = (bf16[2,72,1152]{2,1,0:T(8,128)(2,1)S(1)}, bf16[2,72,1152]{2,1,0:T(8,128)(2,1)S(1)}, u32[]{:S(2)}, u32[]{:S(2)}) collective-permute-start(bf16[2,72,1152]{2,1,0:T(8,128)(2,1)S(1)} %slice.150), channel_id=1, source_target_pairs={{0,34},{2,0},{32,2},{34,32},{1,35},{3,1},{33,3},{35,33},{4,38},{6,... | collective-permute-start | bytes 995336 | tf_op jit(solution)/shard_map/ppermute | solution.py:23
  79.0 14.8 %collective-permute-start.12 = (bf16[2,88,1152]{2,1,0:T(8,128)(2,1)S(1)}, bf16[2,88,1152]{2,1,0:T(8,128)(2,1)S(1)}, u32[]{:S(2)}, u32[]{:S(2)}) collective-permute-start(bf16[2,88,1152]{2,1,0:T(8,128)(2,1)S(1)} %slice.142), channel_id=1, source_target_pairs={{0,64},{64,128},{128,192},{192,0},{1,65},{65,129},{129,193},{193,1... | collective-permute-start | bytes 1216520 | tf_op jit(solution)/shard_map/ppermute | solution.py:23
  79.0 14.8 %collective-permute-start.13 = (bf16[2,88,1152]{2,1,0:T(8,128)(2,1)S(1)}, bf16[2,88,1152]{2,1,0:T(8,128)(2,1)S(1)}, u32[]{:S(2)}, u32[]{:S(2)}) collective-permute-start(bf16[2,88,1152]{2,1,0:T(8,128)(2,1)S(1)} %slice.143), channel_id=1, source_target_pairs={{0,192},{64,0},{128,64},{192,128},{1,193},{65,1},{129,65},{193,129... | collective-permute-start | bytes 1216520 | tf_op jit(solution)/shard_map/ppermute | solution.py:23
  82.3 2.3 %copy-start.1 = (bf16[2048,1152]{1,0:T(8,128)(2,1)S(1)}, bf16[2048,1152]{1,0:T(8,128)(2,1)}, u32[]{:S(2)}) copy-start(bf16[2048,1152]{1,0:T(8,128)(2,1)} %x_ref.1) | copy-start | bytes 14155780
  88.4 15.5 %collective-permute-start.24 = (bf16[2,64,1152]{2,1,0:T(8,128)(2,1)S(1)}, bf16[2,64,1152]{2,1,0:T(8,128)(2,1)S(1)}, u32[]{:S(2)}, u32[]{:S(2)}) collective-permute-start(bf16[2,64,1152]{2,1,0:T(8,128)(2,1)S(1)} %slice.153), channel_id=1, source_target_pairs={{0,64},{64,128},{128,192},{192,0},{1,65},{65,129},{129,193},{193,1... | collective-permute-start | bytes 884744 | tf_op jit(solution)/shard_map/ppermute | solution.py:23
  88.6 15.4 %collective-permute-start.25 = (bf16[2,64,1152]{2,1,0:T(8,128)(2,1)S(1)}, bf16[2,64,1152]{2,1,0:T(8,128)(2,1)S(1)}, u32[]{:S(2)}, u32[]{:S(2)}) collective-permute-start(bf16[2,64,1152]{2,1,0:T(8,128)(2,1)S(1)} %slice.154), channel_id=1, source_target_pairs={{0,192},{64,0},{128,64},{192,128},{1,193},{65,1},{129,65},{193,129... | collective-permute-start | bytes 884744 | tf_op jit(solution)/shard_map/ppermute | solution.py:23
  91.9 12.1 %collective-permute-start.29 = (bf16[2,80,1152]{2,1,0:T(8,128)(2,1)S(1)}, bf16[2,80,1152]{2,1,0:T(8,128)(2,1)S(1)}, u32[]{:S(2)}, u32[]{:S(2)}) collective-permute-start(bf16[2,80,1152]{2,1,0:T(8,128)(2,1)S(1)} %slice.157), channel_id=1, source_target_pairs={{0,2},{2,32},{32,34},{34,0},{1,3},{3,33},{33,35},{35,1},{4,6},{6,3... | collective-permute-start | bytes 1105928 | tf_op jit(solution)/shard_map/ppermute | solution.py:23
  93.9 10.1 %collective-permute-start.30 = (bf16[2,80,1152]{2,1,0:T(8,128)(2,1)S(1)}, bf16[2,80,1152]{2,1,0:T(8,128)(2,1)S(1)}, u32[]{:S(2)}, u32[]{:S(2)}) collective-permute-start(bf16[2,80,1152]{2,1,0:T(8,128)(2,1)S(1)} %slice.158), channel_id=1, source_target_pairs={{0,34},{2,0},{32,2},{34,32},{1,35},{3,1},{33,3},{35,33},{4,38},{6,... | collective-permute-start | bytes 1105928 | tf_op jit(solution)/shard_map/ppermute | solution.py:23
  93.9 8.2 %copy-start.2 = (bf16[1152,1152]{1,0:T(8,128)(2,1)S(1)}, bf16[1152,1152]{1,0:T(8,128)(2,1)}, u32[]{:S(2)}) copy-start(bf16[1152,1152]{1,0:T(8,128)(2,1)} %map_ref.1) | copy-start | bytes 7962628
  108.3 5.7 %collective-permute-start.31 = (bf16[512,1152]{1,0:T(8,128)(2,1)S(1)}, bf16[512,1152]{1,0:T(8,128)(2,1)S(1)}, u32[]{:S(2)}, u32[]{:S(2)}) collective-permute-start(bf16[512,1152]{1,0:T(8,128)(2,1)S(1)} %get-tuple-element.16), channel_id=1, source_target_pairs={{0,1},{1,0},{2,3},{3,2},{4,5},{5,4},{6,7},{7,6},{8,9},{9,8},{10,11... | collective-permute-start | bytes 3538952 | tf_op jit(solution)/shard_map/ppermute | solution.py:308
  108.4 5.6 %collective-permute-start.32 = (bf16[256,1152]{1,0:T(8,128)(2,1)S(1)}, bf16[256,1152]{1,0:T(8,128)(2,1)S(1)}, u32[]{:S(2)}, u32[]{:S(2)}) collective-permute-start(bf16[256,1152]{1,0:T(8,128)(2,1)S(1)} %text.1.text_ref), channel_id=1, source_target_pairs={{0,1},{1,0},{2,3},{3,2},{4,5},{5,4},{6,7},{7,6},{8,9},{9,8},{10,11... | collective-permute-start | bytes 1769480 | tf_op jit(solution)/shard_map/ppermute | solution.py:296
